TPU v7x, 32 devices: a whole 2x2x4 slice. The times are simulated.
32 devices in a mesh: xy: 16 (over z, y, core), gz: 2 (over x).
Axes of the slice: x: 2, y: 2, z: 4, core: 2. Of those that a mesh axis runs over, the one named last changes fastest.
Arguments:
- e_check: float32 [3, 128, 4, 1024], P(None, 'xy', 'gz'), may hold values from -6 to 6
- h_check: float32 [3, 128, 4, 1024], P(None, 'xy', 'gz'), may hold values from -6 to 6
- adj_e: float32 [3, 128, 4, 1024], P(None, 'xy', 'gz'), may hold values from -6 to 6
- adj_h: float32 [3, 128, 4, 1024], P(None, 'xy', 'gz'), may hold values from -6 to 6
- material: int32 [128, 4, 1024], P('xy', 'gz'), may hold values from 0 to 3
- owner: int32 [128, 4, 1024], P('xy', 'gz'), may hold values from 0 to 7
- permittivity: float32 [4], replicated, may hold values from 1 to 4
Outputs:
- adj_e_out: float32 [3, 128, 4, 1024], P(None, 'xy', 'gz')
- adj_h_out: float32 [3, 128, 4, 1024], P(None, 'xy', 'gz')
- height_grad: float32 [8], replicated
All inputs are finite; a program needn't handle non-finite values.
Results may differ from a plain program's by a relative error of at most 0.0003.
Values sent between devices are 32-bit elements; how exact they have to be, the bound alone decides.
A program may use at most 64 MiB of HBM per device.

v0:
```python
import functools

import jax
import jax.numpy as jnp
import numpy as np
from jax import lax
from jax.experimental import pallas as pl
from jax.experimental.pallas import tpu as pltpu
from jax.sharding import PartitionSpec as P

NI = 8
COURANT = 0.5
MESH = pl.DeviceIdType.MESH
SCALES = (-COURANT, 1.0)


def kernel(
    dims, e_hbm, h_hbm, g_hbm, k_hbm, mat_hbm, own_hbm, perm,
    go_ref, ko_ref, grad_ref,
    field, inner, partial, curl_in, outer, mat, own, coef, weight,
    send_xf, send_xl, send_d5, send_d6,
    got_xf, got_zf, got_xl, got_zl, got_d5, got_d6,
    mine, gathered,
    load_sem, send_sem, recv_sem, sum_send, sum_recv,
):
    n_x, n_z, nx, nz, ny, kinds, norm = dims
    total = n_x * n_z
    i = lax.axis_index("xy")
    k = lax.axis_index("gz")
    me = i * n_z + k

    def load(src, dst, slot):
        copies = []
        for z in range(nz):
            src_z = src.at[:, :, z, :] if len(src.shape) == 4 else src.at[:, z, :]
            dst_z = dst.at[:, z] if len(src.shape) == 4 else dst.at[z]
            copies.append(pltpu.make_async_copy(src_z, dst_z, load_sem.at[slot, z]))
        return copies

    loads = [
        load(e_hbm, field.at[0], 0),
        load(h_hbm, inner.at[0], 1),
        load(mat_hbm, mat, 2),
        load(g_hbm, outer, 3),
        load(k_hbm, inner.at[1], 4),
        load(own_hbm, own, 5),
    ]
    for group in loads:
        for copy in group:
            copy.start()

    barrier = pltpu.get_barrier_semaphore()

    def greet(step, carry):
        other = lax.rem(me + step, total)
        pl.semaphore_signal(
            barrier, inc=1, device_id=(other // n_z, lax.rem(other, n_z)), device_id_type=MESH
        )
        return carry

    lax.fori_loop(1, total, greet, 0)

    rows = lax.broadcasted_iota(jnp.int32, (nx, ny), 0)
    lanes = lax.broadcasted_iota(jnp.int32, (nx, ny), 1)
    first_row, last_row = rows == 0, rows == nx - 1
    first_lane, last_lane = lanes == 0, lanes == ny - 1

    def dy(v):
        return jnp.where(last_lane, 0.0, pltpu.roll(v, ny - 1, 1)) - v

    def dx(v):
        return jnp.where(last_row, 0.0, pltpu.roll(v, nx - 1, 0)) - v

    def by(v):
        return v - jnp.where(first_lane, 0.0, pltpu.roll(v, 1, 1))

    def bx(v, row):
        return v - jnp.where(first_row, row, pltpu.roll(v, 1, 0))

    def local_part(q, mag):
        scale = SCALES[q % 2]
        f = field.at[q]
        for z in range(nz):
            fx, fy, fz = f[0, z], f[1, z], f[2, z]
            if z < nz - 1:
                up_x, up_y = f[0, z + 1] - fx, f[1, z + 1] - fy
            else:
                up_x, up_y = -fx, -fy
            lx = mag[0, z] + scale * (dy(fz) - up_y)
            ly = mag[1, z] + scale * (up_x - dx(fz))
            lz = mag[2, z] + scale * (dx(fy) - dy(fx))
            partial[q, 0, z], partial[q, 1, z], partial[q, 2, z] = lx, ly, lz
            send_xf[q, z : z + 1] = fy[0:1]
            send_xf[q, nz + z : nz + z + 1] = fz[0:1]
            send_xl[q, z : z + 1] = ly[nx - 1 : nx]
            send_xl[q, nz + z : nz + z + 1] = lz[nx - 1 : nx]
            if z == 0:
                send_d5[q] = fx[nx - 1 : nx]
            if z == nz - 1:
                send_d6[q] = fz[0:1]

    def messages(q):
        below_x, above_x = i > 0, i < n_x - 1
        below_z, above_z = k > 0, k < n_z - 1
        table = (
            (send_d5.at[q], got_d5.at[q], (i + 1, k - 1), above_x & below_z, below_x & above_z),
            (send_d6.at[q], got_d6.at[q], (i - 1, k + 1), below_x & above_z, above_x & below_z),
            (send_xf.at[q], got_xf.at[q], (i - 1, k), below_x, above_x),
            (send_xl.at[q], got_xl.at[q], (i + 1, k), above_x, below_x),
            (field.at[q, 0:2, 0], got_zf.at[q], (i, k - 1), below_z, above_z),
            (partial.at[q, 0:2, nz - 1], got_zl.at[q], (i, k + 1), above_z, below_z),
        )
        return [
            (
                pltpu.make_async_remote_copy(
                    src_ref=src, dst_ref=dst, send_sem=send_sem.at[q, m],
                    recv_sem=recv_sem.at[q, m], device_id=target, device_id_type=MESH,
                ),
                sends,
                receives,
            )
            for m, (src, dst, target, sends, receives) in enumerate(table)
        ]

    def send(q):
        for copy, sends, _ in messages(q):
            pl.when(sends)(copy.start)

    def receive(q):
        for copy, _, receives in messages(q):
            pl.when(receives)(copy.wait_recv)

    def finish(q, put):
        scale = SCALES[q % 2]
        f, part = field.at[q], partial.at[q]
        not_first_x, not_last_x = i > 0, i < n_x - 1
        not_first_z, not_last_z = k > 0, k < n_z - 1

        def only(cond, v):
            return jnp.where(cond, v, 0.0)

        below_x = only(not_first_z, got_zl[q, 0] - scale * f[1, 0])
        below_y = got_zl[q, 1] + scale * f[0, 0]
        diagonal = only(not_last_x, scale * got_d6[q])
        below_y = only(not_first_z, below_y - jnp.where(last_row, diagonal, 0.0))
        result = []
        for z in range(nz):
            mx, my, mz = part[0, z], part[1, z], part[2, z]
            edge_y = got_xl[q, z : z + 1] - scale * f[2, z, 0:1]
            edge_z = got_xl[q, nz + z : nz + z + 1] + scale * f[1, z, 0:1]
            if z == nz - 1:
                mx = mx - only(not_last_z, scale * got_zf[q, 1])
                my = my + only(not_last_z, scale * got_zf[q, 0])
                edge_y = edge_y + only(not_last_z, scale * got_d5[q])
            edge_y, edge_z = only(not_first_x, edge_y), only(not_first_x, edge_z)
            next_y = only(not_last_x, scale * got_xf[q, z : z + 1])
            next_z = only(not_last_x, scale * got_xf[q, nz + z : nz + z + 1])
            my = my - jnp.where(last_row, next_z, 0.0)
            mz = mz + jnp.where(last_row, next_y, 0.0)
            if put is not None:
                put[0, z], put[1, z], put[2, z] = mx, my, mz
            result.append(
                (
                    by(mz) - (my - below_y),
                    (mx - below_x) - bx(mz, edge_z),
                    bx(my, edge_y) - by(mx),
                )
            )
            below_x, below_y = mx, my
        return result

    for slot in (0, 1):
        for copy in loads[slot]:
            copy.wait()
    local_part(0, inner.at[0])
    for slot in (2, 3, 4):
        for copy in loads[slot]:
            copy.wait()
    for z in range(nz):
        kind = mat[z]
        eps = jnp.full((nx, ny), perm[0], jnp.float32)
        for number in range(1, kinds):
            eps = jnp.where(kind == number, perm[number], eps)
        coef[z] = COURANT / eps
        for c in range(3):
            field[1, c, z] = coef[z] * outer[c, z]
    pl.semaphore_wait(barrier, total - 1)
    send(0)
    local_part(1, inner.at[1])
    send(1)

    receive(0)
    change = finish(0, curl_in.at[0])
    for z in range(nz):
        for c in range(3):
            moved = coef[z] * change[z][c]
            curl_in[2, c, z] = moved
            field[2, c, z] = field[0, c, z] + moved
    local_part(2, curl_in.at[0])
    send(2)

    receive(1)
    change = finish(1, curl_in.at[1])
    for z in range(nz):
        dot = None
        for c in range(3):
            now = outer[c, z] - COURANT * change[z][c]
            inner[1, c, z] = now
            field[3, c, z] = coef[z] * now
            term = now * curl_in[2, c, z]
            dot = term if dot is None else dot + term
        weight[z] = coef[z] * dot
    local_part(3, curl_in.at[1])
    send(3)
    for copy in loads[5]:
        copy.wait()

    receive(2)
    change = finish(2, None)
    sums = [jnp.zeros((nx, 128), jnp.float32)] * NI
    for z in range(nz):
        dot = None
        for c in range(3):
            term = outer[c, z] * (coef[z] * change[z][c])
            dot = term if dot is None else dot + term
        both = weight[z] + coef[z] * dot
        which = own[z]
        for t in range(0, ny, 128):
            part, index = both[:, t : t + 128], which[:, t : t + 128]
            for j in range(NI):
                sums[j] = sums[j] + jnp.where(index == j, part, 0.0)
    lane = lax.broadcasted_iota(jnp.int32, (1, 128), 1)
    line = jnp.zeros((1, 128), jnp.float32)
    for j in range(NI):
        column = jnp.sum(sums[j], axis=0, keepdims=True)
        line = jnp.where(lane == j, jnp.sum(column, axis=1, keepdims=True), line)
    mine[0] = line
    gathered[me] = line

    def share_sum(step, carry):
        other = lax.rem(me + step, total)
        pltpu.make_async_remote_copy(
            src_ref=mine.at[0], dst_ref=gathered.at[me], send_sem=sum_send, recv_sem=sum_recv,
            device_id=(other // n_z, lax.rem(other, n_z)), device_id_type=MESH,
        ).start()
        return carry

    lax.fori_loop(1, total, share_sum, 0)

    receive(3)
    change = finish(3, ko_ref)
    for z in range(nz):
        for c in range(3):
            go_ref[c, z] = inner[1, c, z] - COURANT * change[z][c]
    everyone = gathered.at[0 : total - 1]
    pltpu.make_async_copy(everyone, everyone, sum_recv).wait()
    pltpu.make_async_copy(everyone, everyone, sum_send).wait()
    grad_ref[...] = jnp.sum(gathered[...], axis=0)[:, :NI] / norm
    for q in range(4):
        for copy, sends, _ in messages(q):
            pl.when(sends)(copy.wait_send)

def store(g_ref, h_ref, grad_ref, g_hbm, h_hbm, grad_hbm, sem):
    copies = [pltpu.make_async_copy(grad_ref, grad_hbm, sem.at[2, 0])]
    for z in range(g_ref.shape[1]):
        copies.append(pltpu.make_async_copy(g_ref.at[:, z], g_hbm.at[:, :, z, :], sem.at[0, z]))
        copies.append(pltpu.make_async_copy(h_ref.at[:, z], h_hbm.at[:, :, z, :], sem.at[1, z]))
    for copy in copies:
        copy.start()
    for copy in copies:
        copy.wait()


def solution(mesh):
    n_x, n_z = mesh.shape["xy"], mesh.shape["gz"]

    def body(e_check, h_check, adj_e, adj_h, material, owner, permittivity):
        _, nx, nz, ny = e_check.shape
        cells = nx * n_x * nz * n_z * ny
        norm = np.sqrt(np.float32(cells / NI))
        dims = (n_x, n_z, nx, nz, ny, permittivity.shape[0], norm)
        f32 = jnp.float32
        hbm_spec = pl.BlockSpec(memory_space=pltpu.HBM)
        vmem_spec = pl.BlockSpec(memory_space=pltpu.VMEM)
        block = (3, nz, nx, ny)
        g, h, grad = pl.pallas_call(
            functools.partial(kernel, dims),
            out_shape=(
                pltpu.VMEM(block, f32), pltpu.VMEM(block, f32), pltpu.VMEM((1, NI), f32),
            ),
            in_specs=[hbm_spec] * 6 + [pl.BlockSpec(memory_space=pltpu.SMEM)],
            out_specs=(vmem_spec,) * 3,
            scratch_shapes=[
                pltpu.VMEM((4,) + block, f32),
                pltpu.VMEM((2,) + block, f32),
                pltpu.VMEM((4,) + block, f32),
                pltpu.VMEM((3,) + block, f32),
                pltpu.VMEM(block, f32),
                pltpu.VMEM((nz, nx, ny), jnp.int32),
                pltpu.VMEM((nz, nx, ny), jnp.int32),
                pltpu.VMEM((nz, nx, ny), f32),
                pltpu.VMEM((nz, nx, ny), f32),
                pltpu.VMEM((4, 2 * nz, ny), f32),
                pltpu.VMEM((4, 2 * nz, ny), f32),
                pltpu.VMEM((4, 1, ny), f32),
                pltpu.VMEM((4, 1, ny), f32),
                pltpu.VMEM((4, 2 * nz, ny), f32),
                pltpu.VMEM((4, 2, nx, ny), f32),
                pltpu.VMEM((4, 2 * nz, ny), f32),
                pltpu.VMEM((4, 2, nx, ny), f32),
                pltpu.VMEM((4, 1, ny), f32),
                pltpu.VMEM((4, 1, ny), f32),
                pltpu.VMEM((1, 1, 128), f32),
                pltpu.VMEM((n_x * n_z, 1, 128), f32),
                pltpu.SemaphoreType.DMA((6, nz)),
                pltpu.SemaphoreType.DMA((4, 6)),
                pltpu.SemaphoreType.DMA((4, 6)),
                pltpu.SemaphoreType.DMA,
                pltpu.SemaphoreType.DMA,
            ],
            compiler_params=pltpu.CompilerParams(
                collective_id=0, has_side_effects=True
            ),
            name="yee_adjoint",
        )(e_check, h_check, adj_e, adj_h, material, owner, permittivity)
        g, h, grad = pl.pallas_call(
            store,
            out_shape=(
                jax.ShapeDtypeStruct(e_check.shape, f32),
                jax.ShapeDtypeStruct(e_check.shape, f32),
                jax.ShapeDtypeStruct((1, NI), f32),
            ),
            in_specs=[vmem_spec] * 3,
            out_specs=(hbm_spec,) * 3,
            scratch_shapes=[pltpu.SemaphoreType.DMA((3, nz))],
            compiler_params=pltpu.CompilerParams(vmem_limit_bytes=2**20),
            name="store_outputs",
        )(g, h, grad)
        return g, h, grad.reshape(NI)

    split = P(None, "xy", "gz", None)
    return jax.shard_map(
        body,
        mesh=mesh,
        in_specs=(split,) * 4 + (P("xy", "gz", None),) * 2 + (P(),),
        out_specs=(split, split, P()),
        check_vma=False,
    )
```

profile of v0, /device:TPU:0, one launch (start us, length us, event | category | flops | bytes accessed | tf_op | source)
XLA Modules:
  0.0 21.1 jit_solution(5343006992675583598)
XLA Ops:
  0.6 19.6 %yee_adjoint.1 = (f32[3,2,8,1024]{3,2,1,0:T(8,128)S(1)}, f32[3,2,8,1024]{3,2,1,0:T(8,128)S(1)}, f32[1,8]{1,0:T(1,128)S(1)}) custom-call(f32[3,8,2,1024]{3,2,1,0:T(2,128)} %e_hbm.1, f32[3,8,2,1024]{3,2,1,0:T(2,128)} %h_hbm.1, f32[3,8,2,1024]{3,2,1,0:T(2,128)} %g_hbm.1, f32[3,8,2,1024]{3,2,1,0:T(2,128)} %k_hbm.1, s32[8,2,1024]{2,1,0:T(2,128)} %mat_hbm.1, ...), custom_call_target="tpu_custom_call" | custom-call | tf_op jit(solution)/shard_map/yee_adjoint/pallas_call | solution.py:286
  20.3 0.8 %store_outputs.1 = (f32[3,8,2,1024]{3,2,1,0:T(2,128)}, f32[3,8,2,1024]{3,2,1,0:T(2,128)}, f32[1,8]{1,0:T(1,128)}) custom-call(f32[3,2,8,1024]{3,2,1,0:T(8,128)S(1)} %get-tuple-element.9.g_ref, f32[3,2,8,1024]{3,2,1,0:T(8,128)S(1)} %get-tuple-element.10.h_ref, f32[1,8]{1,0:T(1,128)S(1)} %get-tuple-element.11.grad_ref), custom_call_target="tpu_custom_call" | custom-call | tf_op jit(solution)/shard_map/store_outputs/pallas_call | solution.py:326
where the time goes:
time: 21.2 us; the launch traced here: 21.1 us
  Pallas kernels  20.4 us (96%)
  between operations  0.64 us (3%)
    pallas_call x1, Pallas kernels, body(): pl.pallas_call(functools.partial(kernel, dims), out_shape=(pltpu.VMEM(blo...  19.6 us
    pallas_call x1, Pallas kernels, body(): pl.pallas_call(store, out_shape=(jax.ShapeDtypeStruct(e_check.shape, f32)...  0.8 us

commit v1 on v0

--- a/solution.py
+++ b/solution.py
@@ -21,9 +21,9 @@
     send_xf, send_xl, send_d5, send_d6,
     got_xf, got_zf, got_xl, got_zl, got_d5, got_d6,
     mine, gathered,
-    load_sem, send_sem, recv_sem, sum_send, sum_recv,
+    load_sem, send_sem, recv_sem, sum_send, sum_recv, line_sem,
 ):
-    n_x, n_z, nx, nz, ny, kinds, norm = dims
+    n_x, n_z, nx, nz, ny, kinds, group, norm = dims
     total = n_x * n_z
     i = lax.axis_index("xy")
     k = lax.axis_index("gz")
@@ -45,20 +45,39 @@
         load(k_hbm, inner.at[1], 4),
         load(own_hbm, own, 5),
     ]
-    for group in loads:
-        for copy in group:
+    for copies in loads:
+        for copy in copies:
             copy.start()
 
     barrier = pltpu.get_barrier_semaphore()
-
-    def greet(step, carry):
-        other = lax.rem(me + step, total)
-        pl.semaphore_signal(
-            barrier, inc=1, device_id=(other // n_z, lax.rem(other, n_z)), device_id_type=MESH
-        )
+    line, spot = i // group, lax.rem(i, group)
+    lines, plane = n_x // group, group * n_z
+
+    def signal(sem, x, z):
+        pl.semaphore_signal(sem, inc=1, device_id=(x, z), device_id_type=MESH)
+
+    def greet_plane(step, carry):
+        other = lax.rem(spot * n_z + k + step, plane)
+        signal(barrier, line * group + other // n_z, lax.rem(other, n_z))
         return carry
 
-    lax.fori_loop(1, total, greet, 0)
+    def greet_line(sem):
+        def greet(step, carry):
+            signal(sem, lax.rem(line + step, lines) * group + spot, k)
+            return carry
+
+        lax.fori_loop(1, lines, greet, 0)
+
+    lax.fori_loop(1, plane, greet_plane, 0)
+    greet_line(barrier)
+    greeted = plane - 1 + lines - 1
+    down, up = (spot == 0) & (line > 0), (spot == group - 1) & (line < lines - 1)
+    outside = (
+        (down, -1, 0), (down & (k < n_z - 1), -1, 1), (up, 1, 0), (up & (k > 0), 1, -1),
+    )
+    for cond, step_x, step_z in outside:
+        pl.when(cond)(functools.partial(signal, barrier, i + step_x, k + step_z))
+        greeted = greeted + cond.astype(jnp.int32)
 
     rows = lax.broadcasted_iota(jnp.int32, (nx, ny), 0)
     lanes = lax.broadcasted_iota(jnp.int32, (nx, ny), 1)
@@ -173,6 +192,9 @@
         for copy in loads[slot]:
             copy.wait()
     local_part(0, inner.at[0])
+    pl.semaphore_wait(barrier, greeted)
+    send(0)
+    greet_line(line_sem)
     for slot in (2, 3, 4):
         for copy in loads[slot]:
             copy.wait()
@@ -184,8 +206,6 @@
         coef[z] = COURANT / eps
         for c in range(3):
             field[1, c, z] = coef[z] * outer[c, z]
-    pl.semaphore_wait(barrier, total - 1)
-    send(0)
     local_part(1, inner.at[1])
     send(1)
 
@@ -230,22 +250,24 @@
             for j in range(NI):
                 sums[j] = sums[j] + jnp.where(index == j, part, 0.0)
     lane = lax.broadcasted_iota(jnp.int32, (1, 128), 1)
-    line = jnp.zeros((1, 128), jnp.float32)
+    row = jnp.zeros((1, 128), jnp.float32)
     for j in range(NI):
         column = jnp.sum(sums[j], axis=0, keepdims=True)
-        line = jnp.where(lane == j, jnp.sum(column, axis=1, keepdims=True), line)
-    mine[0] = line
-    gathered[me] = line
+        row = jnp.where(lane == j, jnp.sum(column, axis=1, keepdims=True), row)
+    mine[0] = row
+    gathered[me] = row
+
+    pl.semaphore_wait(line_sem, lines - 1)
 
     def share_sum(step, carry):
-        other = lax.rem(me + step, total)
+        other = jnp.where(step < me, step, step + 1)
         pltpu.make_async_remote_copy(
             src_ref=mine.at[0], dst_ref=gathered.at[me], send_sem=sum_send, recv_sem=sum_recv,
             device_id=(other // n_z, lax.rem(other, n_z)), device_id_type=MESH,
         ).start()
         return carry
 
-    lax.fori_loop(1, total, share_sum, 0)
+    lax.fori_loop(0, total - 1, share_sum, 0)
 
     receive(3)
     change = finish(3, ko_ref)
@@ -278,7 +300,8 @@
         _, nx, nz, ny = e_check.shape
         cells = nx * n_x * nz * n_z * ny
         norm = np.sqrt(np.float32(cells / NI))
-        dims = (n_x, n_z, nx, nz, ny, permittivity.shape[0], norm)
+        group = max(g for g in range(1, n_x + 1) if n_x % g == 0 and g * g <= n_x)
+        dims = (n_x, n_z, nx, nz, ny, permittivity.shape[0], group, norm)
         f32 = jnp.float32
         hbm_spec = pl.BlockSpec(memory_space=pltpu.HBM)
         vmem_spec = pl.BlockSpec(memory_space=pltpu.VMEM)
@@ -317,6 +340,7 @@
                 pltpu.SemaphoreType.DMA((4, 6)),
                 pltpu.SemaphoreType.DMA,
                 pltpu.SemaphoreType.DMA,
+                pltpu.SemaphoreType.REGULAR,
             ],
             compiler_params=pltpu.CompilerParams(
                 collective_id=0, has_side_effects=True

time: 21.2 us -> 20.5 us (0.967)
  Pallas kernels: 20.4 us -> 19.7 us
    pallas_call x1, Pallas kernels: 19.6 us -> 18.9 us  [body(): pl.pallas_call(functools.partial(kernel, dims), out_shape=(pltpu.VMEM(blo...]
where the time goes in v1:
time: 20.5 us; the launch traced here: 20.4 us
  Pallas kernels  19.7 us (96%)
  between operations  0.64 us (3%)
    pallas_call x1, Pallas kernels, body(): pl.pallas_call(functools.partial(kernel, dims), out_shape=(pltpu.VMEM(blo...  18.9 us
    pallas_call x1, Pallas kernels, body(): pl.pallas_call(store, out_shape=(jax.ShapeDtypeStruct(e_check.shape, f32)...  0.8 us

profile of v1, /device:TPU:0, one launch (start us, length us, event | category | flops | bytes accessed | tf_op | source)
XLA Modules:
  0.0 20.4 jit_solution(7337452554693547855)
XLA Ops:
  0.6 18.9 %yee_adjoint.1 = (f32[3,2,8,1024]{3,2,1,0:T(8,128)S(1)}, f32[3,2,8,1024]{3,2,1,0:T(8,128)S(1)}, f32[1,8]{1,0:T(1,128)S(1)}) custom-call(f32[3,8,2,1024]{3,2,1,0:T(2,128)} %e_hbm.1, f32[3,8,2,1024]{3,2,1,0:T(2,128)} %h_hbm.1, f32[3,8,2,1024]{3,2,1,0:T(2,128)} %g_hbm.1, f32[3,8,2,1024]{3,2,1,0:T(2,128)} %k_hbm.1, s32[8,2,1024]{2,1,0:T(2,128)} %mat_hbm.1, ...), custom_call_target="tpu_custom_call" | custom-call | tf_op jit(solution)/shard_map/yee_adjoint/pallas_call | solution.py:309
  19.6 0.8 %store_outputs.1 = (f32[3,8,2,1024]{3,2,1,0:T(2,128)}, f32[3,8,2,1024]{3,2,1,0:T(2,128)}, f32[1,8]{1,0:T(1,128)}) custom-call(f32[3,2,8,1024]{3,2,1,0:T(8,128)S(1)} %get-tuple-element.9.g_ref, f32[3,2,8,1024]{3,2,1,0:T(8,128)S(1)} %get-tuple-element.10.h_ref, f32[1,8]{1,0:T(1,128)S(1)} %get-tuple-element.11.grad_ref), custom_call_target="tpu_custom_call" | custom-call | tf_op jit(solution)/shard_map/store_outputs/pallas_call | solution.py:350

commit v2 on v1

--- a/solution.py
+++ b/solution.py
@@ -1,4 +1,5 @@
 import functools
+import itertools
 
 import jax
 import jax.numpy as jnp
@@ -15,13 +16,13 @@
 
 
 def kernel(
-    dims, e_hbm, h_hbm, g_hbm, k_hbm, mat_hbm, own_hbm, perm,
+    dims, e_hbm, h_hbm, g_hbm, k_hbm, mat_hbm, own_hbm, perm_hbm,
     go_ref, ko_ref, grad_ref,
-    field, inner, partial, curl_in, outer, mat, own, coef, weight,
+    perm, field, inner, partial, curl_in, outer, mat, own, coef, weight,
     send_xf, send_xl, send_d5, send_d6,
     got_xf, got_zf, got_xl, got_zl, got_d5, got_d6,
-    mine, gathered,
-    load_sem, send_sem, recv_sem, sum_send, sum_recv, line_sem,
+    mine, gathered, tally,
+    load_sem, send_sem, recv_sem, sum_send, sum_recv, plane_sem, line_sem,
 ):
     n_x, n_z, nx, nz, ny, kinds, group, norm = dims
     total = n_x * n_z
@@ -30,54 +31,57 @@
     me = i * n_z + k
 
     def load(src, dst, slot):
-        copies = []
         for z in range(nz):
             src_z = src.at[:, :, z, :] if len(src.shape) == 4 else src.at[:, z, :]
             dst_z = dst.at[:, z] if len(src.shape) == 4 else dst.at[z]
-            copies.append(pltpu.make_async_copy(src_z, dst_z, load_sem.at[slot, z]))
-        return copies
-
-    loads = [
-        load(e_hbm, field.at[0], 0),
-        load(h_hbm, inner.at[0], 1),
-        load(mat_hbm, mat, 2),
-        load(g_hbm, outer, 3),
-        load(k_hbm, inner.at[1], 4),
-        load(own_hbm, own, 5),
-    ]
-    for copies in loads:
-        for copy in copies:
-            copy.start()
+            pltpu.make_async_copy(src_z, dst_z, load_sem.at[slot]).start()
+        return pltpu.make_async_copy(dst, dst, load_sem.at[slot])
 
     barrier = pltpu.get_barrier_semaphore()
     line, spot = i // group, lax.rem(i, group)
-    lines, plane = n_x // group, group * n_z
+    lines = n_x // group
 
     def signal(sem, x, z):
         pl.semaphore_signal(sem, inc=1, device_id=(x, z), device_id_type=MESH)
 
-    def greet_plane(step, carry):
-        other = lax.rem(spot * n_z + k + step, plane)
-        signal(barrier, line * group + other // n_z, lax.rem(other, n_z))
-        return carry
-
-    def greet_line(sem):
-        def greet(step, carry):
-            signal(sem, lax.rem(line + step, lines) * group + spot, k)
-            return carry
-
-        lax.fori_loop(1, lines, greet, 0)
-
-    lax.fori_loop(1, plane, greet_plane, 0)
-    greet_line(barrier)
-    greeted = plane - 1 + lines - 1
-    down, up = (spot == 0) & (line > 0), (spot == group - 1) & (line < lines - 1)
-    outside = (
-        (down, -1, 0), (down & (k < n_z - 1), -1, 1), (up, 1, 0), (up & (k > 0), 1, -1),
+    def greet(sem, partners):
+        count = 0
+        for cond, x, z in partners:
+            pl.when(cond)(functools.partial(signal, sem, x, z))
+            count = count + cond.astype(jnp.int32)
+        return count
+
+    def greet_group(sem):
+        for step in range(1, group):
+            signal(sem, line * group + lax.rem(spot + step, group), k)
+        return group - 1
+
+    def greet_line(sem, hop):
+        return greet(
+            sem, ((line >= hop, i - hop * group, k), (line < lines - hop, i + hop * group, k))
+        )
+
+    first, last = (spot == 0) & (line > 0), (spot == group - 1) & (line < lines - 1)
+    greeted = greet(
+        barrier,
+        (
+            (first, i - 1, k), (first & (k < n_z - 1), i - 1, k + 1),
+            (last, i + 1, k), (last & (k > 0), i + 1, k - 1),
+            (~first & (i > 0) & (k < n_z - 1), i - 1, k + 1),
+            (~last & (i < n_x - 1) & (k > 0), i + 1, k - 1),
+        ),
     )
-    for cond, step_x, step_z in outside:
-        pl.when(cond)(functools.partial(signal, barrier, i + step_x, k + step_z))
-        greeted = greeted + cond.astype(jnp.int32)
+    for step in range(1, n_z):
+        signal(barrier, i, lax.rem(k + step, n_z))
+    greeted = greeted + n_z - 1 + greet_group(barrier) + greet_line(barrier, 1)
+
+    loads = [load(e_hbm, field.at[0], 0), load(h_hbm, inner.at[0], 1)]
+    perm_load = pltpu.make_async_copy(perm_hbm, perm, load_sem.at[6])
+    perm_load.start()
+    loads.append(load(mat_hbm, mat, 2))
+    loads.append(load(g_hbm, outer, 3))
+    loads.append(load(k_hbm, inner.at[1], 4))
+    loads.append(load(own_hbm, own, 5))
 
     rows = lax.broadcasted_iota(jnp.int32, (nx, ny), 0)
     lanes = lax.broadcasted_iota(jnp.int32, (nx, ny), 1)
@@ -121,7 +125,7 @@
     def messages(q):
         below_x, above_x = i > 0, i < n_x - 1
         below_z, above_z = k > 0, k < n_z - 1
-        table = (
+        return (
             (send_d5.at[q], got_d5.at[q], (i + 1, k - 1), above_x & below_z, below_x & above_z),
             (send_d6.at[q], got_d6.at[q], (i - 1, k + 1), below_x & above_z, above_x & below_z),
             (send_xf.at[q], got_xf.at[q], (i - 1, k), below_x, above_x),
@@ -129,25 +133,34 @@
             (field.at[q, 0:2, 0], got_zf.at[q], (i, k - 1), below_z, above_z),
             (partial.at[q, 0:2, nz - 1], got_zl.at[q], (i, k + 1), above_z, below_z),
         )
-        return [
-            (
-                pltpu.make_async_remote_copy(
-                    src_ref=src, dst_ref=dst, send_sem=send_sem.at[q, m],
-                    recv_sem=recv_sem.at[q, m], device_id=target, device_id_type=MESH,
-                ),
-                sends,
-                receives,
+
+    def send(q):
+        for src, dst, target, sends, _ in messages(q):
+            copy = pltpu.make_async_remote_copy(
+                src_ref=src, dst_ref=dst, send_sem=send_sem, recv_sem=recv_sem.at[q],
+                device_id=target, device_id_type=MESH,
             )
-            for m, (src, dst, target, sends, receives) in enumerate(table)
-        ]
-
-    def send(q):
-        for copy, sends, _ in messages(q):
             pl.when(sends)(copy.start)
 
+    sides = []
+    for below_x, above_x, below_z, above_z in itertools.product((False, True), repeat=4):
+        if below_x + above_x > n_x - 1 or below_z + above_z > n_z - 1:
+            continue
+        if (n_x > 1 and not below_x + above_x) or (n_z > 1 and not below_z + above_z):
+            continue
+        here = ((i > 0) == below_x) & ((i < n_x - 1) == above_x)
+        here = here & ((k > 0) == below_z) & ((k < n_z - 1) == above_z)
+        length = (above_x & below_z) + (below_x & above_z)
+        length += 2 * nz * (below_x + above_x) + 2 * nx * (below_z + above_z)
+        sides.append((here, length))
+
+    def wait_exchange(sem, times):
+        for here, length in sides:
+            span = tally.at[0 : times * length]
+            pl.when(here)(pltpu.make_async_copy(span, span, sem).wait)
+
     def receive(q):
-        for copy, _, receives in messages(q):
-            pl.when(receives)(copy.wait_recv)
+        wait_exchange(recv_sem.at[q], 1)
 
     def finish(q, put):
         scale = SCALES[q % 2]
@@ -189,15 +202,14 @@
         return result
 
     for slot in (0, 1):
-        for copy in loads[slot]:
-            copy.wait()
+        loads[slot].wait()
     local_part(0, inner.at[0])
     pl.semaphore_wait(barrier, greeted)
     send(0)
-    greet_line(line_sem)
+    greeted = greet_group(plane_sem)
+    perm_load.wait()
     for slot in (2, 3, 4):
-        for copy in loads[slot]:
-            copy.wait()
+        loads[slot].wait()
     for z in range(nz):
         kind = mat[z]
         eps = jnp.full((nx, ny), perm[0], jnp.float32)
@@ -208,6 +220,9 @@
             field[1, c, z] = coef[z] * outer[c, z]
     local_part(1, inner.at[1])
     send(1)
+    pl.semaphore_wait(plane_sem, greeted)
+    hops = [1 << turn for turn in range((lines - 1).bit_length())]
+    greeted = greet_line(line_sem.at[0], hops[0])
 
     receive(0)
     change = finish(0, curl_in.at[0])
@@ -218,6 +233,9 @@
             field[2, c, z] = field[0, c, z] + moved
     local_part(2, curl_in.at[0])
     send(2)
+    for turn, hop in enumerate(hops[1:], 1):
+        pl.semaphore_wait(line_sem.at[turn - 1], greeted)
+        greeted = greet_line(line_sem.at[turn], hop)
 
     receive(1)
     change = finish(1, curl_in.at[1])
@@ -232,8 +250,7 @@
         weight[z] = coef[z] * dot
     local_part(3, curl_in.at[1])
     send(3)
-    for copy in loads[5]:
-        copy.wait()
+    loads[5].wait()
 
     receive(2)
     change = finish(2, None)
@@ -257,7 +274,7 @@
     mine[0] = row
     gathered[me] = row
 
-    pl.semaphore_wait(line_sem, lines - 1)
+    pl.semaphore_wait(line_sem.at[len(hops) - 1], greeted)
 
     def share_sum(step, carry):
         other = jnp.where(step < me, step, step + 1)
@@ -278,19 +295,15 @@
     pltpu.make_async_copy(everyone, everyone, sum_recv).wait()
     pltpu.make_async_copy(everyone, everyone, sum_send).wait()
     grad_ref[...] = jnp.sum(gathered[...], axis=0)[:, :NI] / norm
-    for q in range(4):
-        for copy, sends, _ in messages(q):
-            pl.when(sends)(copy.wait_send)
+    wait_exchange(send_sem, 4)
 
 def store(g_ref, h_ref, grad_ref, g_hbm, h_hbm, grad_hbm, sem):
-    copies = [pltpu.make_async_copy(grad_ref, grad_hbm, sem.at[2, 0])]
+    pltpu.make_async_copy(grad_ref, grad_hbm, sem.at[2]).start()
     for z in range(g_ref.shape[1]):
-        copies.append(pltpu.make_async_copy(g_ref.at[:, z], g_hbm.at[:, :, z, :], sem.at[0, z]))
-        copies.append(pltpu.make_async_copy(h_ref.at[:, z], h_hbm.at[:, :, z, :], sem.at[1, z]))
-    for copy in copies:
-        copy.start()
-    for copy in copies:
-        copy.wait()
+        pltpu.make_async_copy(g_ref.at[:, z], g_hbm.at[:, :, z, :], sem.at[0]).start()
+        pltpu.make_async_copy(h_ref.at[:, z], h_hbm.at[:, :, z, :], sem.at[1]).start()
+    for n, ref in enumerate((g_ref, h_ref, grad_ref)):
+        pltpu.make_async_copy(ref, ref, sem.at[n]).wait()
 
 
 def solution(mesh):
@@ -311,9 +324,10 @@
             out_shape=(
                 pltpu.VMEM(block, f32), pltpu.VMEM(block, f32), pltpu.VMEM((1, NI), f32),
             ),
-            in_specs=[hbm_spec] * 6 + [pl.BlockSpec(memory_space=pltpu.SMEM)],
+            in_specs=[hbm_spec] * 7,
             out_specs=(vmem_spec,) * 3,
             scratch_shapes=[
+                pltpu.SMEM(permittivity.shape, f32),
                 pltpu.VMEM((4,) + block, f32),
                 pltpu.VMEM((2,) + block, f32),
                 pltpu.VMEM((4,) + block, f32),
@@ -335,12 +349,14 @@
                 pltpu.VMEM((4, 1, ny), f32),
                 pltpu.VMEM((1, 1, 128), f32),
                 pltpu.VMEM((n_x * n_z, 1, 128), f32),
-                pltpu.SemaphoreType.DMA((6, nz)),
-                pltpu.SemaphoreType.DMA((4, 6)),
-                pltpu.SemaphoreType.DMA((4, 6)),
+                pltpu.VMEM((8 * (1 + 2 * nz + 2 * nx), 1, ny), f32),
+                pltpu.SemaphoreType.DMA((7,)),
+                pltpu.SemaphoreType.DMA,
+                pltpu.SemaphoreType.DMA((4,)),
                 pltpu.SemaphoreType.DMA,
                 pltpu.SemaphoreType.DMA,
                 pltpu.SemaphoreType.REGULAR,
+                pltpu.SemaphoreType.REGULAR((max(1, (n_x // group - 1).bit_length()),)),
             ],
             compiler_params=pltpu.CompilerParams(
                 collective_id=0, has_side_effects=True
@@ -356,7 +372,7 @@
             ),
             in_specs=[vmem_spec] * 3,
             out_specs=(hbm_spec,) * 3,
-            scratch_shapes=[pltpu.SemaphoreType.DMA((3, nz))],
+            scratch_shapes=[pltpu.SemaphoreType.DMA((3,))],
             compiler_params=pltpu.CompilerParams(vmem_limit_bytes=2**20),
             name="store_outputs",
         )(g, h, grad)

time: 20.5 us -> 19.5 us (0.951)
  Pallas kernels: 19.7 us -> 18.7 us
    pallas_call x1, Pallas kernels: 18.9 us -> 17.9 us  [body(): pl.pallas_call(functools.partial(kernel, dims), out_shape=(pltpu.VMEM(blo...]
where the time goes in v2:
time: 19.5 us; the launch traced here: 19.4 us
  Pallas kernels  18.7 us (96%)
  between operations  0.64 us (3%)
    pallas_call x1, Pallas kernels, body(): pl.pallas_call(functools.partial(kernel, dims), out_shape=(pltpu.VMEM(blo...  17.9 us
    pallas_call x1, Pallas kernels, body(): pl.pallas_call(store, out_shape=(jax.ShapeDtypeStruct(e_check.shape, f32)...  0.77 us

profile of v2, /device:TPU:0, one launch (start us, length us, event | category | flops | bytes accessed | tf_op | source)
XLA Modules:
  0.0 19.4 jit_solution(10525935335144529487)
XLA Ops:
  0.6 17.9 %yee_adjoint.1 = (f32[3,2,8,1024]{3,2,1,0:T(8,128)S(1)}, f32[3,2,8,1024]{3,2,1,0:T(8,128)S(1)}, f32[1,8]{1,0:T(1,128)S(1)}) custom-call(f32[3,8,2,1024]{3,2,1,0:T(2,128)} %e_hbm.1, f32[3,8,2,1024]{3,2,1,0:T(2,128)} %h_hbm.1, f32[3,8,2,1024]{3,2,1,0:T(2,128)} %g_hbm.1, f32[3,8,2,1024]{3,2,1,0:T(2,128)} %k_hbm.1, s32[8,2,1024]{2,1,0:T(2,128)} %mat_hbm.1, ...), custom_call_target="tpu_custom_call" | custom-call | tf_op jit(solution)/shard_map/yee_adjoint/pallas_call | solution.py:322
  18.6 0.8 %store_outputs.1 = (f32[3,8,2,1024]{3,2,1,0:T(2,128)}, f32[3,8,2,1024]{3,2,1,0:T(2,128)}, f32[1,8]{1,0:T(1,128)}) custom-call(f32[3,2,8,1024]{3,2,1,0:T(8,128)S(1)} %get-tuple-element.9.g_ref, f32[3,2,8,1024]{3,2,1,0:T(8,128)S(1)} %get-tuple-element.10.h_ref, f32[1,8]{1,0:T(1,128)S(1)} %get-tuple-element.11.grad_ref), custom_call_target="tpu_custom_call" | custom-call | tf_op jit(solution)/shard_map/store_outputs/pallas_call | solution.py:366

commit v3 on v2

--- a/solution.py
+++ b/solution.py
@@ -12,6 +12,7 @@
 NI = 8
 COURANT = 0.5
 MESH = pl.DeviceIdType.MESH
+LINES, PLANES = slice(0, 4), slice(4, 6)
 SCALES = (-COURANT, 1.0)
 
 
@@ -22,7 +23,8 @@
     send_xf, send_xl, send_d5, send_d6,
     got_xf, got_zf, got_xl, got_zl, got_d5, got_d6,
     mine, gathered, tally,
-    load_sem, send_sem, recv_sem, sum_send, sum_recv, plane_sem, line_sem,
+    load_sem, send_sem, plane_sent, recv_sem, sum_send, sum_recv,
+    plane_sem, line_sem, pair_sem,
 ):
     n_x, n_z, nx, nz, ny, kinds, group, norm = dims
     total = n_x * n_z
@@ -134,11 +136,12 @@
             (partial.at[q, 0:2, nz - 1], got_zl.at[q], (i, k + 1), above_z, below_z),
         )
 
-    def send(q):
-        for src, dst, target, sends, _ in messages(q):
+    def send(q, part=slice(None)):
+        for src, dst, target, sends, _ in messages(q)[part]:
             copy = pltpu.make_async_remote_copy(
-                src_ref=src, dst_ref=dst, send_sem=send_sem, recv_sem=recv_sem.at[q],
-                device_id=target, device_id_type=MESH,
+                src_ref=src, dst_ref=dst, device_id=target, device_id_type=MESH,
+                send_sem=plane_sent.at[q // 2] if part == PLANES and q % 2 == 0 else send_sem,
+                recv_sem=recv_sem.at[q],
             )
             pl.when(sends)(copy.start)
 
@@ -150,17 +153,25 @@
             continue
         here = ((i > 0) == below_x) & ((i < n_x - 1) == above_x)
         here = here & ((k > 0) == below_z) & ((k < n_z - 1) == above_z)
-        length = (above_x & below_z) + (below_x & above_z)
-        length += 2 * nz * (below_x + above_x) + 2 * nx * (below_z + above_z)
-        sides.append((here, length))
-
-    def wait_exchange(sem, times):
-        for here, length in sides:
-            span = tally.at[0 : times * length]
-            pl.when(here)(pltpu.make_async_copy(span, span, sem).wait)
+        length = (above_x & below_z) + (below_x & above_z) + 2 * nz * (below_x + above_x)
+        sides.append((here, length, 2 * nx * (below_z + above_z)))
+
+    def wait_exchange(sem, lines, planes):
+        for here, length, plane in sides:
+            if lines * length + planes * plane:
+                span = tally.at[0 : lines * length + planes * plane]
+                pl.when(here)(pltpu.make_async_copy(span, span, sem).wait)
+
+    def send_after(q):
+        send(q, LINES)
+        wait_exchange(plane_sent.at[q // 2], 0, 1)
+        if n_x % 2 == 0:
+            signal(pair_sem.at[q // 2], i + 1 - 2 * lax.rem(i, 2), k)
+            pl.semaphore_wait(pair_sem.at[q // 2], 1)
+        send(q, PLANES)
 
     def receive(q):
-        wait_exchange(recv_sem.at[q], 1)
+        wait_exchange(recv_sem.at[q], 1, 1)
 
     def finish(q, put):
         scale = SCALES[q % 2]
@@ -205,7 +216,8 @@
         loads[slot].wait()
     local_part(0, inner.at[0])
     pl.semaphore_wait(barrier, greeted)
-    send(0)
+    send(0, LINES)
+    send(0, PLANES)
     greeted = greet_group(plane_sem)
     perm_load.wait()
     for slot in (2, 3, 4):
@@ -219,7 +231,7 @@
         for c in range(3):
             field[1, c, z] = coef[z] * outer[c, z]
     local_part(1, inner.at[1])
-    send(1)
+    send_after(1)
     pl.semaphore_wait(plane_sem, greeted)
     hops = [1 << turn for turn in range((lines - 1).bit_length())]
     greeted = greet_line(line_sem.at[0], hops[0])
@@ -232,7 +244,8 @@
             curl_in[2, c, z] = moved
             field[2, c, z] = field[0, c, z] + moved
     local_part(2, curl_in.at[0])
-    send(2)
+    send(2, LINES)
+    send(2, PLANES)
     for turn, hop in enumerate(hops[1:], 1):
         pl.semaphore_wait(line_sem.at[turn - 1], greeted)
         greeted = greet_line(line_sem.at[turn], hop)
@@ -249,7 +262,7 @@
             dot = term if dot is None else dot + term
         weight[z] = coef[z] * dot
     local_part(3, curl_in.at[1])
-    send(3)
+    send_after(3)
     loads[5].wait()
 
     receive(2)
@@ -295,7 +308,7 @@
     pltpu.make_async_copy(everyone, everyone, sum_recv).wait()
     pltpu.make_async_copy(everyone, everyone, sum_send).wait()
     grad_ref[...] = jnp.sum(gathered[...], axis=0)[:, :NI] / norm
-    wait_exchange(send_sem, 4)
+    wait_exchange(send_sem, 4, 2)
 
 def store(g_ref, h_ref, grad_ref, g_hbm, h_hbm, grad_hbm, sem):
     pltpu.make_async_copy(grad_ref, grad_hbm, sem.at[2]).start()
@@ -352,11 +365,13 @@
                 pltpu.VMEM((8 * (1 + 2 * nz + 2 * nx), 1, ny), f32),
                 pltpu.SemaphoreType.DMA((7,)),
                 pltpu.SemaphoreType.DMA,
+                pltpu.SemaphoreType.DMA((2,)),
                 pltpu.SemaphoreType.DMA((4,)),
                 pltpu.SemaphoreType.DMA,
                 pltpu.SemaphoreType.DMA,
                 pltpu.SemaphoreType.REGULAR,
                 pltpu.SemaphoreType.REGULAR((max(1, (n_x // group - 1).bit_length()),)),
+                pltpu.SemaphoreType.REGULAR((2,)),
             ],
             compiler_params=pltpu.CompilerParams(
                 collective_id=0, has_side_effects=True

time: 19.5 us -> 19 us (0.974)
  Pallas kernels: 18.7 us -> 18.2 us
    pallas_call x1, Pallas kernels: 17.9 us -> 17.4 us  [body(): pl.pallas_call(functools.partial(kernel, dims), out_shape=(pltpu.VMEM(blo...]
where the time goes in v3:
time: 19 us; the launch traced here: 18.8 us
  Pallas kernels  18.2 us (96%)
  between operations  0.64 us (3%)
    pallas_call x1, Pallas kernels, body(): pl.pallas_call(functools.partial(kernel, dims), out_shape=(pltpu.VMEM(blo...  17.4 us
    pallas_call x1, Pallas kernels, body(): pl.pallas_call(store, out_shape=(jax.ShapeDtypeStruct(e_check.shape, f32)...  0.77 us

profile of v3, /device:TPU:0, one launch (start us, length us, event | category | flops | bytes accessed | tf_op | source)
XLA Modules:
  0.0 18.8 jit_solution(5946242546985845180)
XLA Ops:
  0.6 17.4 %yee_adjoint.1 = (f32[3,2,8,1024]{3,2,1,0:T(8,128)S(1)}, f32[3,2,8,1024]{3,2,1,0:T(8,128)S(1)}, f32[1,8]{1,0:T(1,128)S(1)}) custom-call(f32[3,8,2,1024]{3,2,1,0:T(2,128)} %e_hbm.1, f32[3,8,2,1024]{3,2,1,0:T(2,128)} %h_hbm.1, f32[3,8,2,1024]{3,2,1,0:T(2,128)} %g_hbm.1, f32[3,8,2,1024]{3,2,1,0:T(2,128)} %k_hbm.1, s32[8,2,1024]{2,1,0:T(2,128)} %mat_hbm.1, ...), custom_call_target="tpu_custom_call" | custom-call | tf_op jit(solution)/shard_map/yee_adjoint/pallas_call | solution.py:335
  18.0 0.8 %store_outputs.1 = (f32[3,8,2,1024]{3,2,1,0:T(2,128)}, f32[3,8,2,1024]{3,2,1,0:T(2,128)}, f32[1,8]{1,0:T(1,128)}) custom-call(f32[3,2,8,1024]{3,2,1,0:T(8,128)S(1)} %get-tuple-element.9.g_ref, f32[3,2,8,1024]{3,2,1,0:T(8,128)S(1)} %get-tuple-element.10.h_ref, f32[1,8]{1,0:T(1,128)S(1)} %get-tuple-element.11.grad_ref), custom_call_target="tpu_custom_call" | custom-call | tf_op jit(solution)/shard_map/store_outputs/pallas_call | solution.py:381

commit v4 on v3

--- a/solution.py
+++ b/solution.py
@@ -12,7 +12,7 @@
 NI = 8
 COURANT = 0.5
 MESH = pl.DeviceIdType.MESH
-LINES, PLANES = slice(0, 4), slice(4, 6)
+LINES, PLANES = (0, 1, 2, 3), (4, 5, 6, 7)
 SCALES = (-COURANT, 1.0)
 
 
@@ -24,13 +24,14 @@
     got_xf, got_zf, got_xl, got_zl, got_d5, got_d6,
     mine, gathered, tally,
     load_sem, send_sem, plane_sent, recv_sem, sum_send, sum_recv,
-    plane_sem, line_sem, pair_sem,
+    line_sem, pair_sem,
 ):
-    n_x, n_z, nx, nz, ny, kinds, group, norm = dims
+    n_x, n_z, nx, nz, ny, kinds, norm = dims
     total = n_x * n_z
     i = lax.axis_index("xy")
     k = lax.axis_index("gz")
     me = i * n_z + k
+    odd = lax.rem(i, 2) == 1
 
     def load(src, dst, slot):
         for z in range(nz):
@@ -40,8 +41,6 @@
         return pltpu.make_async_copy(dst, dst, load_sem.at[slot])
 
     barrier = pltpu.get_barrier_semaphore()
-    line, spot = i // group, lax.rem(i, group)
-    lines = n_x // group
 
     def signal(sem, x, z):
         pl.semaphore_signal(sem, inc=1, device_id=(x, z), device_id_type=MESH)
@@ -53,31 +52,21 @@
             count = count + cond.astype(jnp.int32)
         return count
 
-    def greet_group(sem):
-        for step in range(1, group):
-            signal(sem, line * group + lax.rem(spot + step, group), k)
-        return group - 1
-
     def greet_line(sem, hop):
-        return greet(
-            sem, ((line >= hop, i - hop * group, k), (line < lines - hop, i + hop * group, k))
-        )
-
-    first, last = (spot == 0) & (line > 0), (spot == group - 1) & (line < lines - 1)
-    greeted = greet(
+        return greet(sem, ((i >= hop, i - hop, k), (i < n_x - hop, i + hop, k)))
+
+    loads = [load(e_hbm, field.at[0], 0), load(h_hbm, inner.at[0], 1)]
+    greeted = greet_line(barrier, 1) + greet(
         barrier,
         (
-            (first, i - 1, k), (first & (k < n_z - 1), i - 1, k + 1),
-            (last, i + 1, k), (last & (k > 0), i + 1, k - 1),
-            (~first & (i > 0) & (k < n_z - 1), i - 1, k + 1),
-            (~last & (i < n_x - 1) & (k > 0), i + 1, k - 1),
+            ((i > 0) & (k < n_z - 1), i - 1, k + 1),
+            ((i < n_x - 1) & (k > 0), i + 1, k - 1),
         ),
     )
     for step in range(1, n_z):
         signal(barrier, i, lax.rem(k + step, n_z))
-    greeted = greeted + n_z - 1 + greet_group(barrier) + greet_line(barrier, 1)
-
-    loads = [load(e_hbm, field.at[0], 0), load(h_hbm, inner.at[0], 1)]
+    greeted = greeted + n_z - 1
+
     perm_load = pltpu.make_async_copy(perm_hbm, perm, load_sem.at[6])
     perm_load.start()
     loads.append(load(mat_hbm, mat, 2))
@@ -115,35 +104,49 @@
             ly = mag[1, z] + scale * (up_x - dx(fz))
             lz = mag[2, z] + scale * (dx(fy) - dy(fx))
             partial[q, 0, z], partial[q, 1, z], partial[q, 2, z] = lx, ly, lz
-            send_xf[q, z : z + 1] = fy[0:1]
-            send_xf[q, nz + z : nz + z + 1] = fz[0:1]
+            if q:
+                send_xf[q, 0, z : z + 1] = fy[0:1]
+                send_xf[q, 1, z : z + 1] = fz[0:1]
             send_xl[q, z : z + 1] = ly[nx - 1 : nx]
             send_xl[q, nz + z : nz + z + 1] = lz[nx - 1 : nx]
-            if z == 0:
+            if q and z == 0:
                 send_d5[q] = fx[nx - 1 : nx]
-            if z == nz - 1:
+            if q and z == nz - 1:
                 send_d6[q] = fz[0:1]
 
     def messages(q):
         below_x, above_x = i > 0, i < n_x - 1
         below_z, above_z = k > 0, k < n_z - 1
+        sources = (
+            (
+                e_hbm.at[0, nx - 1 : nx, 0], e_hbm.at[2, 0:1, nz - 1],
+                e_hbm.at[1:3, 0], e_hbm.at[0:2, :, 0],
+            )
+            if q == 0
+            else (send_d5.at[q], send_d6.at[q], send_xf.at[q], field.at[q, 0:2, 0])
+        )
+        top = partial.at[q, 0:2, nz - 1]
         return (
-            (send_d5.at[q], got_d5.at[q], (i + 1, k - 1), above_x & below_z, below_x & above_z),
-            (send_d6.at[q], got_d6.at[q], (i - 1, k + 1), below_x & above_z, above_x & below_z),
-            (send_xf.at[q], got_xf.at[q], (i - 1, k), below_x, above_x),
-            (send_xl.at[q], got_xl.at[q], (i + 1, k), above_x, below_x),
-            (field.at[q, 0:2, 0], got_zf.at[q], (i, k - 1), below_z, above_z),
-            (partial.at[q, 0:2, nz - 1], got_zl.at[q], (i, k + 1), above_z, below_z),
+            (sources[0], got_d5.at[q], (i + 1, k - 1), above_x & below_z),
+            (sources[1], got_d6.at[q], (i - 1, k + 1), below_x & above_z),
+            (sources[2], got_xf.at[q], (i - 1, k), below_x),
+            (send_xl.at[q], got_xl.at[q], (i + 1, k), above_x),
+            (sources[3].at[0], got_zf.at[q, 0], (i, k - 1), below_z),
+            (top.at[0], got_zl.at[q, 0], (i, k + 1), above_z),
+            (sources[3].at[1], got_zf.at[q, 1], (i, k - 1), below_z),
+            (top.at[1], got_zl.at[q, 1], (i, k + 1), above_z),
         )
 
-    def send(q, part=slice(None)):
-        for src, dst, target, sends, _ in messages(q)[part]:
-            copy = pltpu.make_async_remote_copy(
-                src_ref=src, dst_ref=dst, device_id=target, device_id_type=MESH,
-                send_sem=plane_sent.at[q // 2] if part == PLANES and q % 2 == 0 else send_sem,
-                recv_sem=recv_sem.at[q],
-            )
-            pl.when(sends)(copy.start)
+    def send(q, *chosen):
+        for m, (src, dst, target, sends) in enumerate(messages(q)):
+            if m in chosen:
+                awaited = m in PLANES and q % 2 == 0
+                copy = pltpu.make_async_remote_copy(
+                    src_ref=src, dst_ref=dst, device_id=target, device_id_type=MESH,
+                    send_sem=plane_sent.at[q // 2] if awaited else send_sem,
+                    recv_sem=recv_sem.at[q],
+                )
+                pl.when(sends)(copy.start)
 
     sides = []
     for below_x, above_x, below_z, above_z in itertools.product((False, True), repeat=4):
@@ -154,7 +157,7 @@
         here = ((i > 0) == below_x) & ((i < n_x - 1) == above_x)
         here = here & ((k > 0) == below_z) & ((k < n_z - 1) == above_z)
         length = (above_x & below_z) + (below_x & above_z) + 2 * nz * (below_x + above_x)
-        sides.append((here, length, 2 * nx * (below_z + above_z)))
+        sides.append((here, length, nx * (below_z + above_z)))
 
     def wait_exchange(sem, lines, planes):
         for here, length, plane in sides:
@@ -162,16 +165,8 @@
                 span = tally.at[0 : lines * length + planes * plane]
                 pl.when(here)(pltpu.make_async_copy(span, span, sem).wait)
 
-    def send_after(q):
-        send(q, LINES)
-        wait_exchange(plane_sent.at[q // 2], 0, 1)
-        if n_x % 2 == 0:
-            signal(pair_sem.at[q // 2], i + 1 - 2 * lax.rem(i, 2), k)
-            pl.semaphore_wait(pair_sem.at[q // 2], 1)
-        send(q, PLANES)
-
     def receive(q):
-        wait_exchange(recv_sem.at[q], 1, 1)
+        wait_exchange(recv_sem.at[q], 1, 2)
 
     def finish(q, put):
         scale = SCALES[q % 2]
@@ -196,8 +191,8 @@
                 my = my + only(not_last_z, scale * got_zf[q, 0])
                 edge_y = edge_y + only(not_last_z, scale * got_d5[q])
             edge_y, edge_z = only(not_first_x, edge_y), only(not_first_x, edge_z)
-            next_y = only(not_last_x, scale * got_xf[q, z : z + 1])
-            next_z = only(not_last_x, scale * got_xf[q, nz + z : nz + z + 1])
+            next_y = only(not_last_x, scale * got_xf[q, 0, z : z + 1])
+            next_z = only(not_last_x, scale * got_xf[q, 1, z : z + 1])
             my = my - jnp.where(last_row, next_z, 0.0)
             mz = mz + jnp.where(last_row, next_y, 0.0)
             if put is not None:
@@ -212,13 +207,25 @@
             below_x, below_y = mx, my
         return result
 
+    def open_exchange(*chosen):
+        pl.semaphore_wait(barrier, greeted)
+        send(0, *chosen)
+
+    pl.when(k == n_z - 1)(functools.partial(open_exchange, 4, 6, 0, 1, 2))
     for slot in (0, 1):
         loads[slot].wait()
     local_part(0, inner.at[0])
-    pl.semaphore_wait(barrier, greeted)
-    send(0, LINES)
-    send(0, PLANES)
-    greeted = greet_group(plane_sem)
+    pl.when(k < n_z - 1)(functools.partial(open_exchange, 5, 7, 4, 6, 0, 1, 2))
+    send(0, 3)
+    hops = [1 << turn for turn in range((n_x - 1).bit_length())]
+    told = [greet_line(line_sem.at[0], 1)]
+
+    def tell():
+        turn = len(told)
+        if turn <= len(hops):
+            pl.semaphore_wait(line_sem.at[turn - 1], told[-1])
+            told.append(greet_line(line_sem.at[turn], hops[turn]) if turn < len(hops) else 0)
+
     perm_load.wait()
     for slot in (2, 3, 4):
         loads[slot].wait()
@@ -231,10 +238,11 @@
         for c in range(3):
             field[1, c, z] = coef[z] * outer[c, z]
     local_part(1, inner.at[1])
-    send_after(1)
-    pl.semaphore_wait(plane_sem, greeted)
-    hops = [1 << turn for turn in range((lines - 1).bit_length())]
-    greeted = greet_line(line_sem.at[0], hops[0])
+    send(1, *LINES)
+    pl.when(odd)(functools.partial(wait_exchange, plane_sent.at[0], 0, 2))
+    send(1, *PLANES)
+    tell()
+    tell()
 
     receive(0)
     change = finish(0, curl_in.at[0])
@@ -244,11 +252,8 @@
             curl_in[2, c, z] = moved
             field[2, c, z] = field[0, c, z] + moved
     local_part(2, curl_in.at[0])
-    send(2, LINES)
-    send(2, PLANES)
-    for turn, hop in enumerate(hops[1:], 1):
-        pl.semaphore_wait(line_sem.at[turn - 1], greeted)
-        greeted = greet_line(line_sem.at[turn], hop)
+    send(2, *LINES, *PLANES)
+    tell()
 
     receive(1)
     change = finish(1, curl_in.at[1])
@@ -262,7 +267,16 @@
             dot = term if dot is None else dot + term
         weight[z] = coef[z] * dot
     local_part(3, curl_in.at[1])
-    send_after(3)
+    send(3, *LINES)
+    pl.when(~odd)(functools.partial(send, 3, *PLANES))
+    wait_exchange(plane_sent.at[1], 0, 2)
+    pl.when(~odd & (i < n_x - 1))(functools.partial(signal, pair_sem, i + 1, k))
+
+    @pl.when(odd)
+    def _():
+        pl.semaphore_wait(pair_sem, 1)
+        send(3, *PLANES)
+
     loads[5].wait()
 
     receive(2)
@@ -287,7 +301,8 @@
     mine[0] = row
     gathered[me] = row
 
-    pl.semaphore_wait(line_sem.at[len(hops) - 1], greeted)
+    while len(told) <= len(hops):
+        tell()
 
     def share_sum(step, carry):
         other = jnp.where(step < me, step, step + 1)
@@ -308,7 +323,8 @@
     pltpu.make_async_copy(everyone, everyone, sum_recv).wait()
     pltpu.make_async_copy(everyone, everyone, sum_send).wait()
     grad_ref[...] = jnp.sum(gathered[...], axis=0)[:, :NI] / norm
-    wait_exchange(send_sem, 4, 2)
+    wait_exchange(send_sem, 4, 4)
+    pl.when(~odd)(functools.partial(wait_exchange, plane_sent.at[0], 0, 2))
 
 def store(g_ref, h_ref, grad_ref, g_hbm, h_hbm, grad_hbm, sem):
     pltpu.make_async_copy(grad_ref, grad_hbm, sem.at[2]).start()
@@ -326,8 +342,7 @@
         _, nx, nz, ny = e_check.shape
         cells = nx * n_x * nz * n_z * ny
         norm = np.sqrt(np.float32(cells / NI))
-        group = max(g for g in range(1, n_x + 1) if n_x % g == 0 and g * g <= n_x)
-        dims = (n_x, n_z, nx, nz, ny, permittivity.shape[0], group, norm)
+        dims = (n_x, n_z, nx, nz, ny, permittivity.shape[0], norm)
         f32 = jnp.float32
         hbm_spec = pl.BlockSpec(memory_space=pltpu.HBM)
         vmem_spec = pl.BlockSpec(memory_space=pltpu.VMEM)
@@ -350,11 +365,11 @@
                 pltpu.VMEM((nz, nx, ny), jnp.int32),
                 pltpu.VMEM((nz, nx, ny), f32),
                 pltpu.VMEM((nz, nx, ny), f32),
-                pltpu.VMEM((4, 2 * nz, ny), f32),
+                pltpu.VMEM((4, 2, nz, ny), f32),
                 pltpu.VMEM((4, 2 * nz, ny), f32),
                 pltpu.VMEM((4, 1, ny), f32),
                 pltpu.VMEM((4, 1, ny), f32),
-                pltpu.VMEM((4, 2 * nz, ny), f32),
+                pltpu.VMEM((4, 2, nz, ny), f32),
                 pltpu.VMEM((4, 2, nx, ny), f32),
                 pltpu.VMEM((4, 2 * nz, ny), f32),
                 pltpu.VMEM((4, 2, nx, ny), f32),
@@ -369,9 +384,8 @@
                 pltpu.SemaphoreType.DMA((4,)),
                 pltpu.SemaphoreType.DMA,
                 pltpu.SemaphoreType.DMA,
+                pltpu.SemaphoreType.REGULAR((max(1, (n_x - 1).bit_length()),)),
                 pltpu.SemaphoreType.REGULAR,
-                pltpu.SemaphoreType.REGULAR((max(1, (n_x // group - 1).bit_length()),)),
-                pltpu.SemaphoreType.REGULAR((2,)),
             ],
             compiler_params=pltpu.CompilerParams(
                 collective_id=0, has_side_effects=True

time: 19 us -> 18.6 us (0.979)
  Pallas kernels: 18.2 us -> 17.9 us
    pallas_call x1, Pallas kernels: 17.4 us -> 17.1 us  [body(): pl.pallas_call(functools.partial(kernel, dims), out_shape=(pltpu.VMEM(blo...]
where the time goes in v4:
time: 18.6 us; the launch traced here: 18.5 us
  Pallas kernels  17.9 us (96%)
  between operations  0.64 us (3%)
    pallas_call x1, Pallas kernels, body(): pl.pallas_call(functools.partial(kernel, dims), out_shape=(pltpu.VMEM(blo...  17.1 us
    pallas_call x1, Pallas kernels, body(): pl.pallas_call(store, out_shape=(jax.ShapeDtypeStruct(e_check.shape, f32)...  0.77 us

profile of v4, /device:TPU:0, one launch (start us, length us, event | category | flops | bytes accessed | tf_op | source)
XLA Modules:
  0.0 18.5 jit_solution(10692115787907952343)
XLA Ops:
  0.6 17.1 %yee_adjoint.1 = (f32[3,2,8,1024]{3,2,1,0:T(8,128)S(1)}, f32[3,2,8,1024]{3,2,1,0:T(8,128)S(1)}, f32[1,8]{1,0:T(1,128)S(1)}) custom-call(f32[3,8,2,1024]{3,2,1,0:T(2,128)} %e_hbm.1, f32[3,8,2,1024]{3,2,1,0:T(2,128)} %h_hbm.1, f32[3,8,2,1024]{3,2,1,0:T(2,128)} %g_hbm.1, f32[3,8,2,1024]{3,2,1,0:T(2,128)} %k_hbm.1, s32[8,2,1024]{2,1,0:T(2,128)} %mat_hbm.1, ...), custom_call_target="tpu_custom_call" | custom-call | tf_op jit(solution)/shard_map/yee_adjoint/pallas_call | solution.py:350
  17.7 0.8 %store_outputs.1 = (f32[3,8,2,1024]{3,2,1,0:T(2,128)}, f32[3,8,2,1024]{3,2,1,0:T(2,128)}, f32[1,8]{1,0:T(1,128)}) custom-call(f32[3,2,8,1024]{3,2,1,0:T(8,128)S(1)} %get-tuple-element.9.g_ref, f32[3,2,8,1024]{3,2,1,0:T(8,128)S(1)} %get-tuple-element.10.h_ref, f32[1,8]{1,0:T(1,128)S(1)} %get-tuple-element.11.grad_ref), custom_call_target="tpu_custom_call" | custom-call | tf_op jit(solution)/shard_map/store_outputs/pallas_call | solution.py:395

commit v5 on v4

--- a/solution.py
+++ b/solution.py
@@ -12,7 +12,7 @@
 NI = 8
 COURANT = 0.5
 MESH = pl.DeviceIdType.MESH
-LINES, PLANES = (0, 1, 2, 3), (4, 5, 6, 7)
+LINES, PLANES = (0, 1, 2, 3), (4, 5)
 SCALES = (-COURANT, 1.0)
 
 
@@ -76,43 +76,65 @@
 
     rows = lax.broadcasted_iota(jnp.int32, (nx, ny), 0)
     lanes = lax.broadcasted_iota(jnp.int32, (nx, ny), 1)
-    first_row, last_row = rows == 0, rows == nx - 1
-    first_lane, last_lane = lanes == 0, lanes == ny - 1
-
-    def dy(v):
-        return jnp.where(last_lane, 0.0, pltpu.roll(v, ny - 1, 1)) - v
+
+    def first_row(v):
+        return rows[:, : v.shape[1]] == 0
+
+    def last_row(v):
+        return rows[:, : v.shape[1]] == nx - 1
+
+    def dy(v, whole):
+        width = v.shape[1]
+        later = pltpu.roll(v, width - 1, 1)
+        return jnp.where(lanes[:, :width] == width - 1, 0.0, later) - v if whole else later - v
 
     def dx(v):
-        return jnp.where(last_row, 0.0, pltpu.roll(v, nx - 1, 0)) - v
-
-    def by(v):
-        return v - jnp.where(first_lane, 0.0, pltpu.roll(v, 1, 1))
+        return jnp.where(last_row(v), 0.0, pltpu.roll(v, nx - 1, 0)) - v
+
+    def by(v, whole):
+        earlier = pltpu.roll(v, 1, 1)
+        return v - (jnp.where(lanes[:, : v.shape[1]] == 0, 0.0, earlier) if whole else earlier)
 
     def bx(v, row):
-        return v - jnp.where(first_row, row, pltpu.roll(v, 1, 0))
-
-    def local_part(q, mag):
+        return v - jnp.where(first_row(v), row, pltpu.roll(v, 1, 0))
+
+    def local_part(q, mag, low=0, high=ny):
         scale = SCALES[q % 2]
-        f = field.at[q]
+        end = min(high + 128, ny)
+        inside, keep = pl.ds(low, end - low), pl.ds(low, high - low)
+        width = high - low
+
+        def put(ref, index, v):
+            ref[index + (keep,)] = v[:, :width]
+
         for z in range(nz):
-            fx, fy, fz = f[0, z], f[1, z], f[2, z]
+            fx, fy, fz = (field[q, c, z, :, inside] for c in range(3))
             if z < nz - 1:
-                up_x, up_y = f[0, z + 1] - fx, f[1, z + 1] - fy
+                up_x, up_y = (field[q, c, z + 1, :, inside] for c in range(2))
+                up_x, up_y = up_x - fx, up_y - fy
             else:
                 up_x, up_y = -fx, -fy
-            lx = mag[0, z] + scale * (dy(fz) - up_y)
-            ly = mag[1, z] + scale * (up_x - dx(fz))
-            lz = mag[2, z] + scale * (dx(fy) - dy(fx))
-            partial[q, 0, z], partial[q, 1, z], partial[q, 2, z] = lx, ly, lz
+            whole = end == high
+            lx = mag[0, z, :, inside] + scale * (dy(fz, whole) - up_y)
+            ly = mag[1, z, :, inside] + scale * (up_x - dx(fz))
+            lz = mag[2, z, :, inside] + scale * (dx(fy) - dy(fx, whole))
+            for c, v in enumerate((lx, ly, lz)):
+                put(partial, (q, c, z, slice(None)), v)
             if q:
-                send_xf[q, 0, z : z + 1] = fy[0:1]
-                send_xf[q, 1, z : z + 1] = fz[0:1]
-            send_xl[q, z : z + 1] = ly[nx - 1 : nx]
-            send_xl[q, nz + z : nz + z + 1] = lz[nx - 1 : nx]
+                put(send_xf, (q, 0, slice(z, z + 1)), fy[0:1])
+                put(send_xf, (q, 1, slice(z, z + 1)), fz[0:1])
+            put(send_xl, (q, slice(z, z + 1)), ly[nx - 1 : nx])
+            put(send_xl, (q, slice(nz + z, nz + z + 1)), lz[nx - 1 : nx])
             if q and z == 0:
-                send_d5[q] = fx[nx - 1 : nx]
+                put(send_d5, (q, slice(None)), fx[nx - 1 : nx])
             if q and z == nz - 1:
-                send_d6[q] = fz[0:1]
+                put(send_d6, (q, slice(None)), fz[0:1])
+
+    cut = ny * 4 // 8 // 128 * 128 if ny >= 512 and ny % 128 == 0 else ny
+    spans = [((0, ny),)] * 4
+    if cut < ny:
+        spans[0], spans[2] = ((0, cut), (cut, ny)), ((0, cut - 128), (cut - 128, ny))
+    widths = [high - low for low, high in spans[0]]
 
     def messages(q):
         below_x, above_x = i > 0, i < n_x - 1
@@ -125,28 +147,33 @@
             if q == 0
             else (send_d5.at[q], send_d6.at[q], send_xf.at[q], field.at[q, 0:2, 0])
         )
-        top = partial.at[q, 0:2, nz - 1]
-        return (
+        table = [
             (sources[0], got_d5.at[q], (i + 1, k - 1), above_x & below_z),
             (sources[1], got_d6.at[q], (i - 1, k + 1), below_x & above_z),
             (sources[2], got_xf.at[q], (i - 1, k), below_x),
             (send_xl.at[q], got_xl.at[q], (i + 1, k), above_x),
-            (sources[3].at[0], got_zf.at[q, 0], (i, k - 1), below_z),
-            (top.at[0], got_zl.at[q, 0], (i, k + 1), above_z),
-            (sources[3].at[1], got_zf.at[q, 1], (i, k - 1), below_z),
-            (top.at[1], got_zl.at[q, 1], (i, k + 1), above_z),
-        )
+        ]
+        top = partial.at[q, 0:2, nz - 1]
+        for low, high in spans[q]:
+            keep = pl.ds(low, high - low)
+            for src, got, target, sends in (
+                (sources[3], got_zf, (i, k - 1), below_z), (top, got_zl, (i, k + 1), above_z),
+            ):
+                table.append((src.at[:, :, keep], got.at[q, :, :, keep], target, sends))
+        return table
 
     def send(q, *chosen):
-        for m, (src, dst, target, sends) in enumerate(messages(q)):
-            if m in chosen:
-                awaited = m in PLANES and q % 2 == 0
-                copy = pltpu.make_async_remote_copy(
-                    src_ref=src, dst_ref=dst, device_id=target, device_id_type=MESH,
-                    send_sem=plane_sent.at[q // 2] if awaited else send_sem,
-                    recv_sem=recv_sem.at[q],
-                )
-                pl.when(sends)(copy.start)
+        table = messages(q)
+        for m in chosen:
+            src, dst, target, sends = table[m]
+            sent, late = send_sem, q == 0 and m >= 6
+            if m >= 4 and q % 2 == 0:
+                sent = plane_sent.at[q + late]
+            copy = pltpu.make_async_remote_copy(
+                src_ref=src, dst_ref=dst, device_id=target, device_id_type=MESH,
+                send_sem=sent, recv_sem=recv_sem.at[4 if late else q],
+            )
+            pl.when(sends)(copy.start)
 
     sides = []
     for below_x, above_x, below_z, above_z in itertools.product((False, True), repeat=4):
@@ -157,53 +184,56 @@
         here = ((i > 0) == below_x) & ((i < n_x - 1) == above_x)
         here = here & ((k > 0) == below_z) & ((k < n_z - 1) == above_z)
         length = (above_x & below_z) + (below_x & above_z) + 2 * nz * (below_x + above_x)
-        sides.append((here, length, nx * (below_z + above_z)))
-
-    def wait_exchange(sem, lines, planes):
+        sides.append((here, length, 2 * nx * (below_z + above_z)))
+
+    def wait_exchange(sem, lines, *widths):
         for here, length, plane in sides:
-            if lines * length + planes * plane:
-                span = tally.at[0 : lines * length + planes * plane]
+            count = (lines * length * ny + plane * sum(widths)) // 128
+            if count:
+                span = tally.at[0:count]
                 pl.when(here)(pltpu.make_async_copy(span, span, sem).wait)
 
-    def receive(q):
-        wait_exchange(recv_sem.at[q], 1, 2)
-
-    def finish(q, put):
+    def finish(q, put, low=0, high=ny):
         scale = SCALES[q % 2]
-        f, part = field.at[q], partial.at[q]
+        start = max(low - 128, 0)
+        inside = pl.ds(start, high - start)
         not_first_x, not_last_x = i > 0, i < n_x - 1
         not_first_z, not_last_z = k > 0, k < n_z - 1
 
         def only(cond, v):
             return jnp.where(cond, v, 0.0)
 
-        below_x = only(not_first_z, got_zl[q, 0] - scale * f[1, 0])
-        below_y = got_zl[q, 1] + scale * f[0, 0]
-        diagonal = only(not_last_x, scale * got_d6[q])
-        below_y = only(not_first_z, below_y - jnp.where(last_row, diagonal, 0.0))
+        def f(c, z, part=slice(None)):
+            return field[q, c, z, part, inside]
+
+        bottom_x, bottom_y = got_zl[q, 0, :, inside], got_zl[q, 1, :, inside]
+        below_x = only(not_first_z, bottom_x - scale * f(1, 0))
+        below_y = bottom_y + scale * f(0, 0)
+        diagonal = only(not_last_x, scale * got_d6[q, :, inside])
+        below_y = only(not_first_z, below_y - jnp.where(last_row(below_y), diagonal, 0.0))
         result = []
         for z in range(nz):
-            mx, my, mz = part[0, z], part[1, z], part[2, z]
-            edge_y = got_xl[q, z : z + 1] - scale * f[2, z, 0:1]
-            edge_z = got_xl[q, nz + z : nz + z + 1] + scale * f[1, z, 0:1]
+            mx, my, mz = (partial[q, c, z, :, inside] for c in range(3))
+            edge_y = got_xl[q, z : z + 1, inside] - scale * f(2, z, slice(0, 1))
+            edge_z = got_xl[q, nz + z : nz + z + 1, inside] + scale * f(1, z, slice(0, 1))
             if z == nz - 1:
-                mx = mx - only(not_last_z, scale * got_zf[q, 1])
-                my = my + only(not_last_z, scale * got_zf[q, 0])
-                edge_y = edge_y + only(not_last_z, scale * got_d5[q])
+                mx = mx - only(not_last_z, scale * got_zf[q, 1, :, inside])
+                my = my + only(not_last_z, scale * got_zf[q, 0, :, inside])
+                edge_y = edge_y + only(not_last_z, scale * got_d5[q, :, inside])
             edge_y, edge_z = only(not_first_x, edge_y), only(not_first_x, edge_z)
-            next_y = only(not_last_x, scale * got_xf[q, 0, z : z + 1])
-            next_z = only(not_last_x, scale * got_xf[q, 1, z : z + 1])
-            my = my - jnp.where(last_row, next_z, 0.0)
-            mz = mz + jnp.where(last_row, next_y, 0.0)
+            next_y = only(not_last_x, scale * got_xf[q, 0, z : z + 1, inside])
+            next_z = only(not_last_x, scale * got_xf[q, 1, z : z + 1, inside])
+            my = my - jnp.where(last_row(my), next_z, 0.0)
+            mz = mz + jnp.where(last_row(mz), next_y, 0.0)
+            curl = (
+                by(mz, start == 0) - (my - below_y),
+                (mx - below_x) - bx(mz, edge_z),
+                bx(my, edge_y) - by(mx, start == 0),
+            )
             if put is not None:
-                put[0, z], put[1, z], put[2, z] = mx, my, mz
-            result.append(
-                (
-                    by(mz) - (my - below_y),
-                    (mx - below_x) - bx(mz, edge_z),
-                    bx(my, edge_y) - by(mx),
-                )
-            )
+                for c, v in enumerate((mx, my, mz)):
+                    put[c, z, :, pl.ds(low, high - low)] = v[:, low - start :]
+            result.append([v[:, low - start :] for v in curl])
             below_x, below_y = mx, my
         return result
 
@@ -211,11 +241,14 @@
         pl.semaphore_wait(barrier, greeted)
         send(0, *chosen)
 
-    pl.when(k == n_z - 1)(functools.partial(open_exchange, 4, 6, 0, 1, 2))
+    downs = [4 + 2 * n for n in range(len(widths))]
+    ups = [n + 1 for n in downs]
+    both = [n for pair in zip(ups, downs) for n in pair]
+    pl.when(k == n_z - 1)(functools.partial(open_exchange, 0, 1, *downs, 2))
     for slot in (0, 1):
         loads[slot].wait()
     local_part(0, inner.at[0])
-    pl.when(k < n_z - 1)(functools.partial(open_exchange, 5, 7, 4, 6, 0, 1, 2))
+    pl.when(k < n_z - 1)(functools.partial(open_exchange, 0, 1, *both, 2))
     send(0, 3)
     hops = [1 << turn for turn in range((n_x - 1).bit_length())]
     told = [greet_line(line_sem.at[0], 1)]
@@ -239,23 +272,28 @@
             field[1, c, z] = coef[z] * outer[c, z]
     local_part(1, inner.at[1])
     send(1, *LINES)
-    pl.when(odd)(functools.partial(wait_exchange, plane_sent.at[0], 0, 2))
+    wait_exchange(plane_sent.at[0], 0, widths[0])
+    if len(widths) > 1:
+        pl.when(odd)(functools.partial(wait_exchange, plane_sent.at[1], 0, widths[1]))
     send(1, *PLANES)
     tell()
     tell()
 
-    receive(0)
-    change = finish(0, curl_in.at[0])
-    for z in range(nz):
-        for c in range(3):
-            moved = coef[z] * change[z][c]
-            curl_in[2, c, z] = moved
-            field[2, c, z] = field[0, c, z] + moved
-    local_part(2, curl_in.at[0])
-    send(2, *LINES, *PLANES)
+    for n, (low, high) in enumerate(spans[0]):
+        wait_exchange(recv_sem.at[4 if n else 0], int(n == 0), high - low)
+        change = finish(0, curl_in.at[0], low, high)
+        keep = pl.ds(low, high - low)
+        for z in range(nz):
+            for c in range(3):
+                moved = coef[z, :, keep] * change[z][c]
+                curl_in[2, c, z, :, keep] = moved
+                field[2, c, z, :, keep] = field[0, c, z, :, keep] + moved
+        local_part(2, curl_in.at[0], *spans[2][n])
+        send(2, 4 + 2 * n, 5 + 2 * n)
+    send(2, *LINES)
     tell()
 
-    receive(1)
+    wait_exchange(recv_sem.at[1], 1, ny)
     change = finish(1, curl_in.at[1])
     for z in range(nz):
         dot = None
@@ -269,7 +307,7 @@
     local_part(3, curl_in.at[1])
     send(3, *LINES)
     pl.when(~odd)(functools.partial(send, 3, *PLANES))
-    wait_exchange(plane_sent.at[1], 0, 2)
+    wait_exchange(plane_sent.at[2], 0, ny)
     pl.when(~odd & (i < n_x - 1))(functools.partial(signal, pair_sem, i + 1, k))
 
     @pl.when(odd)
@@ -279,7 +317,7 @@
 
     loads[5].wait()
 
-    receive(2)
+    wait_exchange(recv_sem.at[2], 1, ny)
     change = finish(2, None)
     sums = [jnp.zeros((nx, 128), jnp.float32)] * NI
     for z in range(nz):
@@ -314,7 +352,7 @@
 
     lax.fori_loop(0, total - 1, share_sum, 0)
 
-    receive(3)
+    wait_exchange(recv_sem.at[3], 1, ny)
     change = finish(3, ko_ref)
     for z in range(nz):
         for c in range(3):
@@ -323,8 +361,10 @@
     pltpu.make_async_copy(everyone, everyone, sum_recv).wait()
     pltpu.make_async_copy(everyone, everyone, sum_send).wait()
     grad_ref[...] = jnp.sum(gathered[...], axis=0)[:, :NI] / norm
-    wait_exchange(send_sem, 4, 4)
-    pl.when(~odd)(functools.partial(wait_exchange, plane_sent.at[0], 0, 2))
+    wait_exchange(send_sem, 4, 2 * ny)
+    if len(widths) > 1:
+        pl.when(~odd)(functools.partial(wait_exchange, plane_sent.at[1], 0, widths[1]))
+
 
 def store(g_ref, h_ref, grad_ref, g_hbm, h_hbm, grad_hbm, sem):
     pltpu.make_async_copy(grad_ref, grad_hbm, sem.at[2]).start()
@@ -377,11 +417,11 @@
                 pltpu.VMEM((4, 1, ny), f32),
                 pltpu.VMEM((1, 1, 128), f32),
                 pltpu.VMEM((n_x * n_z, 1, 128), f32),
-                pltpu.VMEM((8 * (1 + 2 * nz + 2 * nx), 1, ny), f32),
+                pltpu.VMEM((8 * (1 + 2 * nz + 2 * nx) * ny // 128, 1, 128), f32),
                 pltpu.SemaphoreType.DMA((7,)),
                 pltpu.SemaphoreType.DMA,
-                pltpu.SemaphoreType.DMA((2,)),
-                pltpu.SemaphoreType.DMA((4,)),
+                pltpu.SemaphoreType.DMA((3,)),
+                pltpu.SemaphoreType.DMA((5,)),
                 pltpu.SemaphoreType.DMA,
                 pltpu.SemaphoreType.DMA,
                 pltpu.SemaphoreType.REGULAR((max(1, (n_x - 1).bit_length()),)),

time: 18.6 us -> 18.3 us (0.984)
  Pallas kernels: 17.9 us -> 17.6 us
    pallas_call x1, Pallas kernels: 17.1 us -> 16.8 us  [body(): pl.pallas_call(functools.partial(kernel, dims), out_shape=(pltpu.VMEM(blo...]
where the time goes in v5:
time: 18.3 us; the launch traced here: 18.2 us
  Pallas kernels  17.6 us (96%)
  between operations  0.64 us (3%)
    pallas_call x1, Pallas kernels, body(): pl.pallas_call(functools.partial(kernel, dims), out_shape=(pltpu.VMEM(blo...  16.8 us
    pallas_call x1, Pallas kernels, body(): pl.pallas_call(store, out_shape=(jax.ShapeDtypeStruct(e_check.shape, f32)...  0.77 us

profile of v5, /device:TPU:0, one launch (start us, length us, event | category | flops | bytes accessed | tf_op | source)
XLA Modules:
  0.0 18.2 jit_solution(5269189900610070189)
XLA Ops:
  0.6 16.8 %yee_adjoint.1 = (f32[3,2,8,1024]{3,2,1,0:T(8,128)S(1)}, f32[3,2,8,1024]{3,2,1,0:T(8,128)S(1)}, f32[1,8]{1,0:T(1,128)S(1)}) custom-call(f32[3,8,2,1024]{3,2,1,0:T(2,128)} %e_hbm.1, f32[3,8,2,1024]{3,2,1,0:T(2,128)} %h_hbm.1, f32[3,8,2,1024]{3,2,1,0:T(2,128)} %g_hbm.1, f32[3,8,2,1024]{3,2,1,0:T(2,128)} %k_hbm.1, s32[8,2,1024]{2,1,0:T(2,128)} %mat_hbm.1, ...), custom_call_target="tpu_custom_call" | custom-call | tf_op jit(solution)/shard_map/yee_adjoint/pallas_call | solution.py:390
  17.4 0.8 %store_outputs.1 = (f32[3,8,2,1024]{3,2,1,0:T(2,128)}, f32[3,8,2,1024]{3,2,1,0:T(2,128)}, f32[1,8]{1,0:T(1,128)}) custom-call(f32[3,2,8,1024]{3,2,1,0:T(8,128)S(1)} %get-tuple-element.9.g_ref, f32[3,2,8,1024]{3,2,1,0:T(8,128)S(1)} %get-tuple-element.10.h_ref, f32[1,8]{1,0:T(1,128)S(1)} %get-tuple-element.11.grad_ref), custom_call_target="tpu_custom_call" | custom-call | tf_op jit(solution)/shard_map/store_outputs/pallas_call | solution.py:435

commit v6 on v5

--- a/solution.py
+++ b/solution.py
@@ -23,8 +23,9 @@
     send_xf, send_xl, send_d5, send_d6,
     got_xf, got_zf, got_xl, got_zl, got_d5, got_d6,
     mine, gathered, tally,
+    pair_zf, pair_zl, pair_give, pair_weight, pair_own,
     load_sem, send_sem, plane_sent, recv_sem, sum_send, sum_recv,
-    line_sem, pair_sem,
+    line_sem, pair_sem, pair_sent, pair_got,
 ):
     n_x, n_z, nx, nz, ny, kinds, norm = dims
     total = n_x * n_z
@@ -130,10 +131,12 @@
             if q and z == nz - 1:
                 put(send_d6, (q, slice(None)), fz[0:1])
 
-    cut = ny * 4 // 8 // 128 * 128 if ny >= 512 and ny % 128 == 0 else ny
     spans = [((0, ny),)] * 4
-    if cut < ny:
-        spans[0], spans[2] = ((0, cut), (cut, ny)), ((0, cut - 128), (cut - 128, ny))
+    if ny % 1024 == 0:
+        cuts = [ny // 8 * n for n in (4,)]
+        spans[0] = tuple(zip([0] + cuts, cuts + [ny]))
+        ahead = [n - 128 for n in cuts]
+        spans[2] = tuple(zip([0] + ahead, ahead + [ny]))
     widths = [high - low for low, high in spans[0]]
 
     def messages(q):
@@ -156,22 +159,28 @@
         top = partial.at[q, 0:2, nz - 1]
         for low, high in spans[q]:
             keep = pl.ds(low, high - low)
-            for src, got, target, sends in (
-                (sources[3], got_zf, (i, k - 1), below_z), (top, got_zl, (i, k + 1), above_z),
-            ):
-                table.append((src.at[:, :, keep], got.at[q, :, :, keep], target, sends))
+            planes = [
+                (sources[3], got_zf.at[q], (i, k - 1), below_z),
+                (top, got_zl.at[q], (i, k + 1), above_z),
+            ]
+            if q == 2:
+                planes = [(*row[:3], row[3] & odd) for row in planes]
+                planes.append((sources[3], pair_zf, (i + 1, k - 1), below_z & ~odd))
+                planes.append((top, pair_zl, (i + 1, k + 1), above_z & ~odd))
+            for src, got, target, sends in planes:
+                table.append((src.at[:, :, keep], got.at[:, :, keep], target, sends))
         return table
 
     def send(q, *chosen):
         table = messages(q)
         for m in chosen:
             src, dst, target, sends = table[m]
-            sent, late = send_sem, q == 0 and m >= 6
+            sent, late = send_sem, max(m // 2 - 2, 0) if q == 0 else 0
             if m >= 4 and q % 2 == 0:
-                sent = plane_sent.at[q + late]
+                sent = plane_sent.at[q + min(late, 1)]
             copy = pltpu.make_async_remote_copy(
                 src_ref=src, dst_ref=dst, device_id=target, device_id_type=MESH,
-                send_sem=sent, recv_sem=recv_sem.at[4 if late else q],
+                send_sem=sent, recv_sem=recv_sem.at[3 + late if late else q],
             )
             pl.when(sends)(copy.start)
 
@@ -184,10 +193,11 @@
         here = ((i > 0) == below_x) & ((i < n_x - 1) == above_x)
         here = here & ((k > 0) == below_z) & ((k < n_z - 1) == above_z)
         length = (above_x & below_z) + (below_x & above_z) + 2 * nz * (below_x + above_x)
-        sides.append((here, length, 2 * nx * (below_z + above_z)))
-
-    def wait_exchange(sem, lines, *widths):
-        for here, length, plane in sides:
+        sides.append((here, length, nx * below_z, nx * above_z))
+
+    def wait_exchange(sem, lines, *widths, pair=False):
+        for here, length, below, above in sides:
+            plane = 3 * below + 4 * above if pair else 2 * (below + above)
             count = (lines * length * ny + plane * sum(widths)) // 128
             if count:
                 span = tally.at[0:count]
@@ -207,6 +217,11 @@
             return field[q, c, z, part, inside]
 
         bottom_x, bottom_y = got_zl[q, 0, :, inside], got_zl[q, 1, :, inside]
+        top_x, top_y = got_zf[q, 0, :, inside], got_zf[q, 1, :, inside]
+        if q == 2:
+            bottom_x, bottom_y, top_x, top_y = (
+                only(odd, v) for v in (bottom_x, bottom_y, top_x, top_y)
+            )
         below_x = only(not_first_z, bottom_x - scale * f(1, 0))
         below_y = bottom_y + scale * f(0, 0)
         diagonal = only(not_last_x, scale * got_d6[q, :, inside])
@@ -217,8 +232,8 @@
             edge_y = got_xl[q, z : z + 1, inside] - scale * f(2, z, slice(0, 1))
             edge_z = got_xl[q, nz + z : nz + z + 1, inside] + scale * f(1, z, slice(0, 1))
             if z == nz - 1:
-                mx = mx - only(not_last_z, scale * got_zf[q, 1, :, inside])
-                my = my + only(not_last_z, scale * got_zf[q, 0, :, inside])
+                mx = mx - only(not_last_z, scale * top_y)
+                my = my + only(not_last_z, scale * top_x)
                 edge_y = edge_y + only(not_last_z, scale * got_d5[q, :, inside])
             edge_y, edge_z = only(not_first_x, edge_y), only(not_first_x, edge_z)
             next_y = only(not_last_x, scale * got_xf[q, 0, z : z + 1, inside])
@@ -272,15 +287,35 @@
             field[1, c, z] = coef[z] * outer[c, z]
     local_part(1, inner.at[1])
     send(1, *LINES)
+    loads[5].wait()
+
+    @pl.when(~odd)
+    def _():
+        for c in range(3):
+            pair_give[c] = coef[nz - 1] * field[1, c, nz - 1]
+        for c in range(2):
+            pair_give[3 + c] = coef[0] * field[1, c, 0]
+        for src, dst, wanted in (
+            (pair_give.at[0:3], pair_weight.at[0:3], k < n_z - 1),
+            (own.at[nz - 1], pair_own.at[0], k < n_z - 1),
+            (pair_give.at[3:5], pair_weight.at[3:5], k > 0),
+            (own.at[0], pair_own.at[1], k > 0),
+        ):
+            copy = pltpu.make_async_remote_copy(
+                src_ref=src, dst_ref=dst, device_id=(i + 1, k), device_id_type=MESH,
+                send_sem=pair_sent, recv_sem=pair_got,
+            )
+            pl.when(wanted)(copy.start)
+
     wait_exchange(plane_sent.at[0], 0, widths[0])
     if len(widths) > 1:
-        pl.when(odd)(functools.partial(wait_exchange, plane_sent.at[1], 0, widths[1]))
+        pl.when(odd)(functools.partial(wait_exchange, plane_sent.at[1], 0, *widths[1:]))
     send(1, *PLANES)
     tell()
     tell()
 
     for n, (low, high) in enumerate(spans[0]):
-        wait_exchange(recv_sem.at[4 if n else 0], int(n == 0), high - low)
+        wait_exchange(recv_sem.at[3 + n if n else 0], int(n == 0), high - low)
         change = finish(0, curl_in.at[0], low, high)
         keep = pl.ds(low, high - low)
         for z in range(nz):
@@ -289,8 +324,10 @@
                 curl_in[2, c, z, :, keep] = moved
                 field[2, c, z, :, keep] = field[0, c, z, :, keep] + moved
         local_part(2, curl_in.at[0], *spans[2][n])
-        send(2, 4 + 2 * n, 5 + 2 * n)
-    send(2, *LINES)
+        if n == len(widths) - 1:
+            send(2, 0, 1)
+        send(2, *range(4 + 4 * n, 8 + 4 * n))
+    send(2, 2, 3)
     tell()
 
     wait_exchange(recv_sem.at[1], 1, ny)
@@ -315,18 +352,28 @@
         pl.semaphore_wait(pair_sem, 1)
         send(3, *PLANES)
 
-    loads[5].wait()
-
-    wait_exchange(recv_sem.at[2], 1, ny)
+    @pl.when(odd)
+    def _():
+        wait_exchange(pair_got, 0, ny, pair=True)
+        wait_exchange(recv_sem.at[2], 1, 2 * ny)
+
+    pl.when(~odd)(functools.partial(wait_exchange, recv_sem.at[2], 1))
     change = finish(2, None)
     sums = [jnp.zeros((nx, 128), jnp.float32)] * NI
+    planes = []
     for z in range(nz):
         dot = None
         for c in range(3):
             term = outer[c, z] * (coef[z] * change[z][c])
             dot = term if dot is None else dot + term
-        both = weight[z] + coef[z] * dot
-        which = own[z]
+        planes.append((weight[z] + coef[z] * dot, own[z]))
+    push_x, push_y = -SCALES[0] * pair_zf[1], SCALES[0] * pair_zf[0]
+    turn = bx(push_y, 0.0) - by(push_x, True)
+    above = pair_weight[1] * push_x - pair_weight[0] * push_y + pair_weight[2] * turn
+    below = pair_weight[3] * pair_zl[1] - pair_weight[4] * pair_zl[0]
+    planes.append((jnp.where(odd & (k < n_z - 1), above, 0.0), pair_own[0]))
+    planes.append((jnp.where(odd & (k > 0), below, 0.0), pair_own[1]))
+    for both, which in planes:
         for t in range(0, ny, 128):
             part, index = both[:, t : t + 128], which[:, t : t + 128]
             for j in range(NI):
@@ -362,8 +409,9 @@
     pltpu.make_async_copy(everyone, everyone, sum_send).wait()
     grad_ref[...] = jnp.sum(gathered[...], axis=0)[:, :NI] / norm
     wait_exchange(send_sem, 4, 2 * ny)
+    pl.when(~odd)(functools.partial(wait_exchange, pair_sent, 0, ny, pair=True))
     if len(widths) > 1:
-        pl.when(~odd)(functools.partial(wait_exchange, plane_sent.at[1], 0, widths[1]))
+        pl.when(~odd)(functools.partial(wait_exchange, plane_sent.at[1], 0, *widths[1:]))
 
 
 def store(g_ref, h_ref, grad_ref, g_hbm, h_hbm, grad_hbm, sem):
@@ -418,6 +466,11 @@
                 pltpu.VMEM((1, 1, 128), f32),
                 pltpu.VMEM((n_x * n_z, 1, 128), f32),
                 pltpu.VMEM((8 * (1 + 2 * nz + 2 * nx) * ny // 128, 1, 128), f32),
+                pltpu.VMEM((2, nx, ny), f32),
+                pltpu.VMEM((2, nx, ny), f32),
+                pltpu.VMEM((5, nx, ny), f32),
+                pltpu.VMEM((5, nx, ny), f32),
+                pltpu.VMEM((2, nx, ny), jnp.int32),
                 pltpu.SemaphoreType.DMA((7,)),
                 pltpu.SemaphoreType.DMA,
                 pltpu.SemaphoreType.DMA((3,)),
@@ -426,6 +479,8 @@
                 pltpu.SemaphoreType.DMA,
                 pltpu.SemaphoreType.REGULAR((max(1, (n_x - 1).bit_length()),)),
                 pltpu.SemaphoreType.REGULAR,
+                pltpu.SemaphoreType.DMA,
+                pltpu.SemaphoreType.DMA,
             ],
             compiler_params=pltpu.CompilerParams(
                 collective_id=0, has_side_effects=True

time: 18.3 us -> 17.9 us (0.978)
  Pallas kernels: 17.6 us -> 17.1 us
    pallas_call x1, Pallas kernels: 16.8 us -> 16.4 us  [body(): pl.pallas_call(functools.partial(kernel, dims), out_shape=(pltpu.VMEM(blo...]
where the time goes in v6:
time: 17.9 us; the launch traced here: 17.8 us
  Pallas kernels  17.1 us (96%)
  between operations  0.64 us (4%)
    pallas_call x1, Pallas kernels, body(): pl.pallas_call(functools.partial(kernel, dims), out_shape=(pltpu.VMEM(blo...  16.4 us
    pallas_call x1, Pallas kernels, body(): pl.pallas_call(store, out_shape=(jax.ShapeDtypeStruct(e_check.shape, f32)...  0.77 us

profile of v6, /device:TPU:0, one launch (start us, length us, event | category | flops | bytes accessed | tf_op | source)
XLA Modules:
  0.0 17.8 jit_solution(15410860094130556224)
XLA Ops:
  0.6 16.4 %yee_adjoint.1 = (f32[3,2,8,1024]{3,2,1,0:T(8,128)S(1)}, f32[3,2,8,1024]{3,2,1,0:T(8,128)S(1)}, f32[1,8]{1,0:T(1,128)S(1)}) custom-call(f32[3,8,2,1024]{3,2,1,0:T(2,128)} %e_hbm.1, f32[3,8,2,1024]{3,2,1,0:T(2,128)} %h_hbm.1, f32[3,8,2,1024]{3,2,1,0:T(2,128)} %g_hbm.1, f32[3,8,2,1024]{3,2,1,0:T(2,128)} %k_hbm.1, s32[8,2,1024]{2,1,0:T(2,128)} %mat_hbm.1, ...), custom_call_target="tpu_custom_call" | custom-call | tf_op jit(solution)/shard_map/yee_adjoint/pallas_call | solution.py:438
  17.0 0.8 %store_outputs.1 = (f32[3,8,2,1024]{3,2,1,0:T(2,128)}, f32[3,8,2,1024]{3,2,1,0:T(2,128)}, f32[1,8]{1,0:T(1,128)}) custom-call(f32[3,2,8,1024]{3,2,1,0:T(8,128)S(1)} %get-tuple-element.9.g_ref, f32[3,2,8,1024]{3,2,1,0:T(8,128)S(1)} %get-tuple-element.10.h_ref, f32[1,8]{1,0:T(1,128)S(1)} %get-tuple-element.11.grad_ref), custom_call_target="tpu_custom_call" | custom-call | tf_op jit(solution)/shard_map/store_outputs/pallas_call | solution.py:490

commit v7 on v6

--- a/solution.py
+++ b/solution.py
@@ -23,9 +23,9 @@
     send_xf, send_xl, send_d5, send_d6,
     got_xf, got_zf, got_xl, got_zl, got_d5, got_d6,
     mine, gathered, tally,
-    pair_zf, pair_zl, pair_give, pair_weight, pair_own,
-    load_sem, send_sem, plane_sent, recv_sem, sum_send, sum_recv,
-    line_sem, pair_sem, pair_sent, pair_got,
+    pair_zf, pair_zl, pair_give, pair_weight, pair_own, portion,
+    load_sem, send_sem, plane_sent, recv_sem, sum_recv,
+    line_sem, pair_sem,
 ):
     n_x, n_z, nx, nz, ny, kinds, norm = dims
     total = n_x * n_z
@@ -37,9 +37,14 @@
     def load(src, dst, slot):
         for z in range(nz):
             src_z = src.at[:, :, z, :] if len(src.shape) == 4 else src.at[:, z, :]
-            dst_z = dst.at[:, z] if len(src.shape) == 4 else dst.at[z]
+            dst_z = dst.at[:, z] if len(dst.shape) == 4 else dst.at[z]
             pltpu.make_async_copy(src_z, dst_z, load_sem.at[slot]).start()
-        return pltpu.make_async_copy(dst, dst, load_sem.at[slot])
+
+    def wait_blocks(sem, count):
+        span = tally.at[0:count]
+        pltpu.make_async_copy(span, span, sem).wait()
+
+    cell_blocks = nx * nz * ny // 128
 
     barrier = pltpu.get_barrier_semaphore()
 
@@ -56,7 +61,8 @@
     def greet_line(sem, hop):
         return greet(sem, ((i >= hop, i - hop, k), (i < n_x - hop, i + hop, k)))
 
-    loads = [load(e_hbm, field.at[0], 0), load(h_hbm, inner.at[0], 1)]
+    load(e_hbm, field.at[0], 0)
+    load(h_hbm, inner.at[0], 0)
     greeted = greet_line(barrier, 1) + greet(
         barrier,
         (
@@ -68,12 +74,12 @@
         signal(barrier, i, lax.rem(k + step, n_z))
     greeted = greeted + n_z - 1
 
-    perm_load = pltpu.make_async_copy(perm_hbm, perm, load_sem.at[6])
+    perm_load = pltpu.make_async_copy(perm_hbm, perm, load_sem.at[2])
     perm_load.start()
-    loads.append(load(mat_hbm, mat, 2))
-    loads.append(load(g_hbm, outer, 3))
-    loads.append(load(k_hbm, inner.at[1], 4))
-    loads.append(load(own_hbm, own, 5))
+    load(mat_hbm, mat, 1)
+    load(g_hbm, outer, 1)
+    load(k_hbm, inner.at[1], 1)
+    load(own_hbm, own, 1)
 
     rows = lax.broadcasted_iota(jnp.int32, (nx, ny), 0)
     lanes = lax.broadcasted_iota(jnp.int32, (nx, ny), 1)
@@ -195,10 +201,10 @@
         length = (above_x & below_z) + (below_x & above_z) + 2 * nz * (below_x + above_x)
         sides.append((here, length, nx * below_z, nx * above_z))
 
-    def wait_exchange(sem, lines, *widths, pair=False):
+    def wait_exchange(sem, lines, *widths, pairs=0, extra=0):
         for here, length, below, above in sides:
-            plane = 3 * below + 4 * above if pair else 2 * (below + above)
-            count = (lines * length * ny + plane * sum(widths)) // 128
+            count = lines * length * ny + 2 * (below + above) * sum(widths)
+            count = (count + pairs * (3 * below + 4 * above) * ny) // 128 + extra
             if count:
                 span = tally.at[0:count]
                 pl.when(here)(pltpu.make_async_copy(span, span, sem).wait)
@@ -260,8 +266,7 @@
     ups = [n + 1 for n in downs]
     both = [n for pair in zip(ups, downs) for n in pair]
     pl.when(k == n_z - 1)(functools.partial(open_exchange, 0, 1, *downs, 2))
-    for slot in (0, 1):
-        loads[slot].wait()
+    wait_blocks(load_sem.at[0], 6 * cell_blocks)
     local_part(0, inner.at[0])
     pl.when(k < n_z - 1)(functools.partial(open_exchange, 0, 1, *both, 2))
     send(0, 3)
@@ -275,8 +280,7 @@
             told.append(greet_line(line_sem.at[turn], hops[turn]) if turn < len(hops) else 0)
 
     perm_load.wait()
-    for slot in (2, 3, 4):
-        loads[slot].wait()
+    wait_blocks(load_sem.at[1], 8 * cell_blocks)
     for z in range(nz):
         kind = mat[z]
         eps = jnp.full((nx, ny), perm[0], jnp.float32)
@@ -287,8 +291,6 @@
             field[1, c, z] = coef[z] * outer[c, z]
     local_part(1, inner.at[1])
     send(1, *LINES)
-    loads[5].wait()
-
     @pl.when(~odd)
     def _():
         for c in range(3):
@@ -303,7 +305,7 @@
         ):
             copy = pltpu.make_async_remote_copy(
                 src_ref=src, dst_ref=dst, device_id=(i + 1, k), device_id_type=MESH,
-                send_sem=pair_sent, recv_sem=pair_got,
+                send_sem=send_sem, recv_sem=recv_sem.at[2],
             )
             pl.when(wanted)(copy.start)
 
@@ -344,19 +346,7 @@
     local_part(3, curl_in.at[1])
     send(3, *LINES)
     pl.when(~odd)(functools.partial(send, 3, *PLANES))
-    wait_exchange(plane_sent.at[2], 0, ny)
-    pl.when(~odd & (i < n_x - 1))(functools.partial(signal, pair_sem, i + 1, k))
-
-    @pl.when(odd)
-    def _():
-        pl.semaphore_wait(pair_sem, 1)
-        send(3, *PLANES)
-
-    @pl.when(odd)
-    def _():
-        wait_exchange(pair_got, 0, ny, pair=True)
-        wait_exchange(recv_sem.at[2], 1, 2 * ny)
-
+    pl.when(odd)(functools.partial(wait_exchange, recv_sem.at[2], 1, 2 * ny, pairs=1))
     pl.when(~odd)(functools.partial(wait_exchange, recv_sem.at[2], 1))
     change = finish(2, None)
     sums = [jnp.zeros((nx, 128), jnp.float32)] * NI
@@ -367,22 +357,40 @@
             term = outer[c, z] * (coef[z] * change[z][c])
             dot = term if dot is None else dot + term
         planes.append((weight[z] + coef[z] * dot, own[z]))
-    push_x, push_y = -SCALES[0] * pair_zf[1], SCALES[0] * pair_zf[0]
-    turn = bx(push_y, 0.0) - by(push_x, True)
-    above = pair_weight[1] * push_x - pair_weight[0] * push_y + pair_weight[2] * turn
-    below = pair_weight[3] * pair_zl[1] - pair_weight[4] * pair_zl[0]
-    planes.append((jnp.where(odd & (k < n_z - 1), above, 0.0), pair_own[0]))
-    planes.append((jnp.where(odd & (k > 0), below, 0.0), pair_own[1]))
     for both, which in planes:
         for t in range(0, ny, 128):
             part, index = both[:, t : t + 128], which[:, t : t + 128]
             for j in range(NI):
                 sums[j] = sums[j] + jnp.where(index == j, part, 0.0)
-    lane = lax.broadcasted_iota(jnp.int32, (1, 128), 1)
-    row = jnp.zeros((1, 128), jnp.float32)
     for j in range(NI):
-        column = jnp.sum(sums[j], axis=0, keepdims=True)
-        row = jnp.where(lane == j, jnp.sum(column, axis=1, keepdims=True), row)
+        portion[j] = sums[j]
+
+    def include(both, which):
+        for j in range(NI):
+            one = portion[j]
+            for t in range(0, ny, 128):
+                one = one + jnp.where(which[:, t : t + 128] == j, both[:, t : t + 128], 0.0)
+            portion[j] = one
+
+    @pl.when(odd & (k < n_z - 1))
+    def _():
+        push_x, push_y = -SCALES[0] * pair_zf[1], SCALES[0] * pair_zf[0]
+        turn = bx(push_y, 0.0) - by(push_x, True)
+        above = pair_weight[1] * push_x - pair_weight[0] * push_y + pair_weight[2] * turn
+        include(above, pair_own[0])
+
+    @pl.when(odd & (k > 0))
+    def _():
+        below = pair_weight[3] * pair_zl[1] - pair_weight[4] * pair_zl[0]
+        include(below, pair_own[1])
+
+    lane = lax.broadcasted_iota(jnp.int32, (NI, 128), 1)
+    number = lax.broadcasted_iota(jnp.int32, (NI, 128), 0)
+    table = jnp.zeros((NI, 128), jnp.float32)
+    for j in range(NI):
+        table = jnp.where(number == j, jnp.sum(portion[j], axis=0, keepdims=True), table)
+    table = jnp.where(lane == number, jnp.sum(table, axis=1, keepdims=True), 0.0)
+    row = jnp.sum(table, axis=0, keepdims=True)
     mine[0] = row
     gathered[me] = row
 
@@ -392,26 +400,37 @@
     def share_sum(step, carry):
         other = jnp.where(step < me, step, step + 1)
         pltpu.make_async_remote_copy(
-            src_ref=mine.at[0], dst_ref=gathered.at[me], send_sem=sum_send, recv_sem=sum_recv,
+            src_ref=mine.at[0], dst_ref=gathered.at[me], send_sem=send_sem, recv_sem=sum_recv,
             device_id=(other // n_z, lax.rem(other, n_z)), device_id_type=MESH,
         ).start()
         return carry
 
     lax.fori_loop(0, total - 1, share_sum, 0)
+
+    wait_exchange(plane_sent.at[2], 0, ny)
+    pl.when(~odd & (i < n_x - 1))(functools.partial(signal, pair_sem, i + 1, k))
+
+    @pl.when(odd)
+    def _():
+        pl.semaphore_wait(pair_sem, 1)
+        send(3, *PLANES)
 
     wait_exchange(recv_sem.at[3], 1, ny)
     change = finish(3, ko_ref)
     for z in range(nz):
         for c in range(3):
             go_ref[c, z] = inner[1, c, z] - COURANT * change[z][c]
+    for parity, pairs in ((odd, 0), (~odd, 1)):
+        pl.when(parity)(
+            functools.partial(
+                wait_exchange, send_sem, 4, 2 * ny, pairs=pairs, extra=total - 1
+            )
+        )
+    if len(widths) > 1:
+        pl.when(~odd)(functools.partial(wait_exchange, plane_sent.at[1], 0, *widths[1:]))
     everyone = gathered.at[0 : total - 1]
     pltpu.make_async_copy(everyone, everyone, sum_recv).wait()
-    pltpu.make_async_copy(everyone, everyone, sum_send).wait()
     grad_ref[...] = jnp.sum(gathered[...], axis=0)[:, :NI] / norm
-    wait_exchange(send_sem, 4, 2 * ny)
-    pl.when(~odd)(functools.partial(wait_exchange, pair_sent, 0, ny, pair=True))
-    if len(widths) > 1:
-        pl.when(~odd)(functools.partial(wait_exchange, plane_sent.at[1], 0, *widths[1:]))
 
 
 def store(g_ref, h_ref, grad_ref, g_hbm, h_hbm, grad_hbm, sem):
@@ -465,22 +484,20 @@
                 pltpu.VMEM((4, 1, ny), f32),
                 pltpu.VMEM((1, 1, 128), f32),
                 pltpu.VMEM((n_x * n_z, 1, 128), f32),
-                pltpu.VMEM((8 * (1 + 2 * nz + 2 * nx) * ny // 128, 1, 128), f32),
+                pltpu.VMEM((16 * (1 + 2 * nz + 2 * nx) * ny // 128 + n_x * n_z, 1, 128), f32),
                 pltpu.VMEM((2, nx, ny), f32),
                 pltpu.VMEM((2, nx, ny), f32),
                 pltpu.VMEM((5, nx, ny), f32),
                 pltpu.VMEM((5, nx, ny), f32),
                 pltpu.VMEM((2, nx, ny), jnp.int32),
-                pltpu.SemaphoreType.DMA((7,)),
+                pltpu.VMEM((NI, nx, 128), f32),
+                pltpu.SemaphoreType.DMA((3,)),
                 pltpu.SemaphoreType.DMA,
                 pltpu.SemaphoreType.DMA((3,)),
                 pltpu.SemaphoreType.DMA((5,)),
                 pltpu.SemaphoreType.DMA,
-                pltpu.SemaphoreType.DMA,
                 pltpu.SemaphoreType.REGULAR((max(1, (n_x - 1).bit_length()),)),
                 pltpu.SemaphoreType.REGULAR,
-                pltpu.SemaphoreType.DMA,
-                pltpu.SemaphoreType.DMA,
             ],
             compiler_params=pltpu.CompilerParams(
                 collective_id=0, has_side_effects=True

time: 17.9 us -> 17.9 us (level)
  no operation moved by 1% of the time
where the time goes in v7:
time: 17.9 us; the launch traced here: 17.7 us
  Pallas kernels  17.1 us (96%)
  between operations  0.64 us (4%)
    pallas_call x1, Pallas kernels, body(): pl.pallas_call(functools.partial(kernel, dims), out_shape=(pltpu.VMEM(blo...  16.3 us
    pallas_call x1, Pallas kernels, body(): pl.pallas_call(store, out_shape=(jax.ShapeDtypeStruct(e_check.shape, f32)...  0.77 us

profile of v7, /device:TPU:0, one launch (start us, length us, event | category | flops | bytes accessed | tf_op | source)
XLA Modules:
  0.0 17.7 jit_solution(9390437144260938069)
XLA Ops:
  0.6 16.3 %yee_adjoint.1 = (f32[3,2,8,1024]{3,2,1,0:T(8,128)S(1)}, f32[3,2,8,1024]{3,2,1,0:T(8,128)S(1)}, f32[1,8]{1,0:T(1,128)S(1)}) custom-call(f32[3,8,2,1024]{3,2,1,0:T(2,128)} %e_hbm.1, f32[3,8,2,1024]{3,2,1,0:T(2,128)} %h_hbm.1, f32[3,8,2,1024]{3,2,1,0:T(2,128)} %g_hbm.1, f32[3,8,2,1024]{3,2,1,0:T(2,128)} %k_hbm.1, s32[8,2,1024]{2,1,0:T(2,128)} %mat_hbm.1, ...), custom_call_target="tpu_custom_call" | custom-call | tf_op jit(solution)/shard_map/yee_adjoint/pallas_call | solution.py:457
  16.9 0.8 %store_outputs.1 = (f32[3,8,2,1024]{3,2,1,0:T(2,128)}, f32[3,8,2,1024]{3,2,1,0:T(2,128)}, f32[1,8]{1,0:T(1,128)}) custom-call(f32[3,2,8,1024]{3,2,1,0:T(8,128)S(1)} %get-tuple-element.9.g_ref, f32[3,2,8,1024]{3,2,1,0:T(8,128)S(1)} %get-tuple-element.10.h_ref, f32[1,8]{1,0:T(1,128)S(1)} %get-tuple-element.11.grad_ref), custom_call_target="tpu_custom_call" | custom-call | tf_op jit(solution)/shard_map/store_outputs/pallas_call | solution.py:507

commit v8 on v7

--- a/solution.py
+++ b/solution.py
@@ -61,7 +61,10 @@
     def greet_line(sem, hop):
         return greet(sem, ((i >= hop, i - hop, k), (i < n_x - hop, i + hop, k)))
 
-    load(e_hbm, field.at[0], 0)
+    pltpu.make_async_copy(e_hbm.at[0:2, :, 0], field.at[0, 0:2, 0], load_sem.at[3]).start()
+    pltpu.make_async_copy(e_hbm.at[2, :, 0], field.at[0, 2, 0], load_sem.at[0]).start()
+    for z in range(1, nz):
+        pltpu.make_async_copy(e_hbm.at[:, :, z], field.at[0, :, z], load_sem.at[0]).start()
     load(h_hbm, inner.at[0], 0)
     greeted = greet_line(barrier, 1) + greet(
         barrier,
@@ -151,7 +154,7 @@
         sources = (
             (
                 e_hbm.at[0, nx - 1 : nx, 0], e_hbm.at[2, 0:1, nz - 1],
-                e_hbm.at[1:3, 0], e_hbm.at[0:2, :, 0],
+                e_hbm.at[1:3, 0], field.at[0, 0:2, 0],
             )
             if q == 0
             else (send_d5.at[q], send_d6.at[q], send_xf.at[q], field.at[q, 0:2, 0])
@@ -184,9 +187,12 @@
             sent, late = send_sem, max(m // 2 - 2, 0) if q == 0 else 0
             if m >= 4 and q % 2 == 0:
                 sent = plane_sent.at[q + min(late, 1)]
+            landing = 3 + late if late else q
+            if q == 2 and m >= 4 and m % 4 > 1:
+                landing = 5
             copy = pltpu.make_async_remote_copy(
                 src_ref=src, dst_ref=dst, device_id=target, device_id_type=MESH,
-                send_sem=sent, recv_sem=recv_sem.at[3 + late if late else q],
+                send_sem=sent, recv_sem=recv_sem.at[landing],
             )
             pl.when(sends)(copy.start)
 
@@ -265,8 +271,16 @@
     downs = [4 + 2 * n for n in range(len(widths))]
     ups = [n + 1 for n in downs]
     both = [n for pair in zip(ups, downs) for n in pair]
-    pl.when(k == n_z - 1)(functools.partial(open_exchange, 0, 1, *downs, 2))
-    wait_blocks(load_sem.at[0], 6 * cell_blocks)
+    @pl.when(k == n_z - 1)
+    def _():
+        open_exchange(0, 1)
+        wait_blocks(load_sem.at[3], 2 * nx * ny // 128)
+        pl.when(~odd)(functools.partial(send, 0, *downs))
+        send(0, 2)
+
+    wait_blocks(load_sem.at[0], 6 * cell_blocks - 2 * nx * ny // 128)
+    pl.when(k < n_z - 1)(functools.partial(wait_blocks, load_sem.at[3], 2 * nx * ny // 128))
+    pl.when(odd & (k == n_z - 1))(functools.partial(send, 0, *downs))
     local_part(0, inner.at[0])
     pl.when(k < n_z - 1)(functools.partial(open_exchange, 0, 1, *both, 2))
     send(0, 3)
@@ -314,7 +328,6 @@
         pl.when(odd)(functools.partial(wait_exchange, plane_sent.at[1], 0, *widths[1:]))
     send(1, *PLANES)
     tell()
-    tell()
 
     for n, (low, high) in enumerate(spans[0]):
         wait_exchange(recv_sem.at[3 + n if n else 0], int(n == 0), high - low)
@@ -329,6 +342,8 @@
         if n == len(widths) - 1:
             send(2, 0, 1)
         send(2, *range(4 + 4 * n, 8 + 4 * n))
+        if n == 0:
+            tell()
     send(2, 2, 3)
     tell()
 
@@ -346,7 +361,7 @@
     local_part(3, curl_in.at[1])
     send(3, *LINES)
     pl.when(~odd)(functools.partial(send, 3, *PLANES))
-    pl.when(odd)(functools.partial(wait_exchange, recv_sem.at[2], 1, 2 * ny, pairs=1))
+    pl.when(odd)(functools.partial(wait_exchange, recv_sem.at[2], 1, ny, pairs=1))
     pl.when(~odd)(functools.partial(wait_exchange, recv_sem.at[2], 1))
     change = finish(2, None)
     sums = [jnp.zeros((nx, 128), jnp.float32)] * NI
@@ -371,6 +386,8 @@
             for t in range(0, ny, 128):
                 one = one + jnp.where(which[:, t : t + 128] == j, both[:, t : t + 128], 0.0)
             portion[j] = one
+
+    pl.when(odd)(functools.partial(wait_exchange, recv_sem.at[5], 0, ny))
 
     @pl.when(odd & (k < n_z - 1))
     def _():
@@ -491,10 +508,10 @@
                 pltpu.VMEM((5, nx, ny), f32),
                 pltpu.VMEM((2, nx, ny), jnp.int32),
                 pltpu.VMEM((NI, nx, 128), f32),
-                pltpu.SemaphoreType.DMA((3,)),
+                pltpu.SemaphoreType.DMA((4,)),
                 pltpu.SemaphoreType.DMA,
                 pltpu.SemaphoreType.DMA((3,)),
-                pltpu.SemaphoreType.DMA((5,)),
+                pltpu.SemaphoreType.DMA((6,)),
                 pltpu.SemaphoreType.DMA,
                 pltpu.SemaphoreType.REGULAR((max(1, (n_x - 1).bit_length()),)),
                 pltpu.SemaphoreType.REGULAR,

time: 17.9 us -> 17.8 us (level)
  no operation moved by 1% of the time
where the time goes in v8:
time: 17.8 us; the launch traced here: 17.6 us
  Pallas kernels  17 us (96%)
  between operations  0.64 us (4%)
    pallas_call x1, Pallas kernels, body(): pl.pallas_call(functools.partial(kernel, dims), out_shape=(pltpu.VMEM(blo...  16.2 us
    pallas_call x1, Pallas kernels, body(): pl.pallas_call(store, out_shape=(jax.ShapeDtypeStruct(e_check.shape, f32)...  0.77 us

profile of v8, /device:TPU:0, one launch (start us, length us, event | category | flops | bytes accessed | tf_op | source)
XLA Modules:
  0.0 17.6 jit_solution(15638489907581770712)
XLA Ops:
  0.6 16.2 %yee_adjoint.1 = (f32[3,2,8,1024]{3,2,1,0:T(8,128)S(1)}, f32[3,2,8,1024]{3,2,1,0:T(8,128)S(1)}, f32[1,8]{1,0:T(1,128)S(1)}) custom-call(f32[3,8,2,1024]{3,2,1,0:T(2,128)} %e_hbm.1, f32[3,8,2,1024]{3,2,1,0:T(2,128)} %h_hbm.1, f32[3,8,2,1024]{3,2,1,0:T(2,128)} %g_hbm.1, f32[3,8,2,1024]{3,2,1,0:T(2,128)} %k_hbm.1, s32[8,2,1024]{2,1,0:T(2,128)} %mat_hbm.1, ...), custom_call_target="tpu_custom_call" | custom-call | tf_op jit(solution)/shard_map/yee_adjoint/pallas_call | solution.py:474
  16.8 0.8 %store_outputs.1 = (f32[3,8,2,1024]{3,2,1,0:T(2,128)}, f32[3,8,2,1024]{3,2,1,0:T(2,128)}, f32[1,8]{1,0:T(1,128)}) custom-call(f32[3,2,8,1024]{3,2,1,0:T(8,128)S(1)} %get-tuple-element.9.g_ref, f32[3,2,8,1024]{3,2,1,0:T(8,128)S(1)} %get-tuple-element.10.h_ref, f32[1,8]{1,0:T(1,128)S(1)} %get-tuple-element.11.grad_ref), custom_call_target="tpu_custom_call" | custom-call | tf_op jit(solution)/shard_map/store_outputs/pallas_call | solution.py:524

commit v9 on v8

--- a/solution.py
+++ b/solution.py
@@ -61,10 +61,7 @@
     def greet_line(sem, hop):
         return greet(sem, ((i >= hop, i - hop, k), (i < n_x - hop, i + hop, k)))
 
-    pltpu.make_async_copy(e_hbm.at[0:2, :, 0], field.at[0, 0:2, 0], load_sem.at[3]).start()
-    pltpu.make_async_copy(e_hbm.at[2, :, 0], field.at[0, 2, 0], load_sem.at[0]).start()
-    for z in range(1, nz):
-        pltpu.make_async_copy(e_hbm.at[:, :, z], field.at[0, :, z], load_sem.at[0]).start()
+    load(e_hbm, field.at[0], 0)
     load(h_hbm, inner.at[0], 0)
     greeted = greet_line(barrier, 1) + greet(
         barrier,
@@ -154,7 +151,7 @@
         sources = (
             (
                 e_hbm.at[0, nx - 1 : nx, 0], e_hbm.at[2, 0:1, nz - 1],
-                e_hbm.at[1:3, 0], field.at[0, 0:2, 0],
+                e_hbm.at[1:3, 0], e_hbm.at[0:2, :, 0],
             )
             if q == 0
             else (send_d5.at[q], send_d6.at[q], send_xf.at[q], field.at[q, 0:2, 0])
@@ -274,12 +271,10 @@
     @pl.when(k == n_z - 1)
     def _():
         open_exchange(0, 1)
-        wait_blocks(load_sem.at[3], 2 * nx * ny // 128)
         pl.when(~odd)(functools.partial(send, 0, *downs))
         send(0, 2)
 
-    wait_blocks(load_sem.at[0], 6 * cell_blocks - 2 * nx * ny // 128)
-    pl.when(k < n_z - 1)(functools.partial(wait_blocks, load_sem.at[3], 2 * nx * ny // 128))
+    wait_blocks(load_sem.at[0], 6 * cell_blocks)
     pl.when(odd & (k == n_z - 1))(functools.partial(send, 0, *downs))
     local_part(0, inner.at[0])
     pl.when(k < n_z - 1)(functools.partial(open_exchange, 0, 1, *both, 2))
@@ -508,7 +503,7 @@
                 pltpu.VMEM((5, nx, ny), f32),
                 pltpu.VMEM((2, nx, ny), jnp.int32),
                 pltpu.VMEM((NI, nx, 128), f32),
-                pltpu.SemaphoreType.DMA((4,)),
+                pltpu.SemaphoreType.DMA((3,)),
                 pltpu.SemaphoreType.DMA,
                 pltpu.SemaphoreType.DMA((3,)),
                 pltpu.SemaphoreType.DMA((6,)),

time: 17.8 us -> 17.7 us (level)
  no operation moved by 1% of the time
where the time goes in v9:
time: 17.7 us; the launch traced here: 17.5 us
  Pallas kernels  16.9 us (95%)
  between operations  0.64 us (4%)
    pallas_call x1, Pallas kernels, body(): pl.pallas_call(functools.partial(kernel, dims), out_shape=(pltpu.VMEM(blo...  16.1 us
    pallas_call x1, Pallas kernels, body(): pl.pallas_call(store, out_shape=(jax.ShapeDtypeStruct(e_check.shape, f32)...  0.77 us

profile of v9, /device:TPU:0, one launch (start us, length us, event | category | flops | bytes accessed | tf_op | source)
XLA Modules:
  0.0 17.5 jit_solution(7145872415862197313)
XLA Ops:
  0.6 16.1 %yee_adjoint.1 = (f32[3,2,8,1024]{3,2,1,0:T(8,128)S(1)}, f32[3,2,8,1024]{3,2,1,0:T(8,128)S(1)}, f32[1,8]{1,0:T(1,128)S(1)}) custom-call(f32[3,8,2,1024]{3,2,1,0:T(2,128)} %e_hbm.1, f32[3,8,2,1024]{3,2,1,0:T(2,128)} %h_hbm.1, f32[3,8,2,1024]{3,2,1,0:T(2,128)} %g_hbm.1, f32[3,8,2,1024]{3,2,1,0:T(2,128)} %k_hbm.1, s32[8,2,1024]{2,1,0:T(2,128)} %mat_hbm.1, ...), custom_call_target="tpu_custom_call" | custom-call | tf_op jit(solution)/shard_map/yee_adjoint/pallas_call | solution.py:469
  16.7 0.8 %store_outputs.1 = (f32[3,8,2,1024]{3,2,1,0:T(2,128)}, f32[3,8,2,1024]{3,2,1,0:T(2,128)}, f32[1,8]{1,0:T(1,128)}) custom-call(f32[3,2,8,1024]{3,2,1,0:T(8,128)S(1)} %get-tuple-element.9.g_ref, f32[3,2,8,1024]{3,2,1,0:T(8,128)S(1)} %get-tuple-element.10.h_ref, f32[1,8]{1,0:T(1,128)S(1)} %get-tuple-element.11.grad_ref), custom_call_target="tpu_custom_call" | custom-call | tf_op jit(solution)/shard_map/store_outputs/pallas_call | solution.py:519

commit v10 on v9

--- a/solution.py
+++ b/solution.py
@@ -61,8 +61,8 @@
     def greet_line(sem, hop):
         return greet(sem, ((i >= hop, i - hop, k), (i < n_x - hop, i + hop, k)))
 
-    load(e_hbm, field.at[0], 0)
-    load(h_hbm, inner.at[0], 0)
+    for step in range(1, n_z):
+        signal(barrier, i, lax.rem(k + step, n_z))
     greeted = greet_line(barrier, 1) + greet(
         barrier,
         (
@@ -70,9 +70,9 @@
             ((i < n_x - 1) & (k > 0), i + 1, k - 1),
         ),
     )
-    for step in range(1, n_z):
-        signal(barrier, i, lax.rem(k + step, n_z))
     greeted = greeted + n_z - 1
+    load(e_hbm, field.at[0], 0)
+    load(h_hbm, inner.at[0], 0)
 
     perm_load = pltpu.make_async_copy(perm_hbm, perm, load_sem.at[2])
     perm_load.start()

time: 17.7 us -> 17.6 us (level)
  no operation moved by 1% of the time
where the time goes in v10:
time: 17.6 us; the launch traced here: 17.5 us
  Pallas kernels  16.8 us (95%)
  between operations  0.64 us (4%)
    pallas_call x1, Pallas kernels, body(): pl.pallas_call(functools.partial(kernel, dims), out_shape=(pltpu.VMEM(blo...  16.1 us
    pallas_call x1, Pallas kernels, body(): pl.pallas_call(store, out_shape=(jax.ShapeDtypeStruct(e_check.shape, f32)...  0.77 us

profile of v10, /device:TPU:0, one launch (start us, length us, event | category | flops | bytes accessed | tf_op | source)
XLA Modules:
  0.0 17.5 jit_solution(16356116151997685386)
XLA Ops:
  0.6 16.1 %yee_adjoint.1 = (f32[3,2,8,1024]{3,2,1,0:T(8,128)S(1)}, f32[3,2,8,1024]{3,2,1,0:T(8,128)S(1)}, f32[1,8]{1,0:T(1,128)S(1)}) custom-call(f32[3,8,2,1024]{3,2,1,0:T(2,128)} %e_hbm.1, f32[3,8,2,1024]{3,2,1,0:T(2,128)} %h_hbm.1, f32[3,8,2,1024]{3,2,1,0:T(2,128)} %g_hbm.1, f32[3,8,2,1024]{3,2,1,0:T(2,128)} %k_hbm.1, s32[8,2,1024]{2,1,0:T(2,128)} %mat_hbm.1, ...), custom_call_target="tpu_custom_call" | custom-call | tf_op jit(solution)/shard_map/yee_adjoint/pallas_call | solution.py:469
  16.7 0.8 %store_outputs.1 = (f32[3,8,2,1024]{3,2,1,0:T(2,128)}, f32[3,8,2,1024]{3,2,1,0:T(2,128)}, f32[1,8]{1,0:T(1,128)}) custom-call(f32[3,2,8,1024]{3,2,1,0:T(8,128)S(1)} %get-tuple-element.9.g_ref, f32[3,2,8,1024]{3,2,1,0:T(8,128)S(1)} %get-tuple-element.10.h_ref, f32[1,8]{1,0:T(1,128)S(1)} %get-tuple-element.11.grad_ref), custom_call_target="tpu_custom_call" | custom-call | tf_op jit(solution)/shard_map/store_outputs/pallas_call | solution.py:519
